TPU v7x, 32 devices: a 4x2x2 block of a 4x4x8 slice. The times are simulated.
32 devices in a mesh: dp: 4 (over y, z), ep: 8 (over x, core).
Axes of the slice: x: 4, y: 2, z: 2, core: 2. Of those that a mesh axis runs over, the one named last changes fastest.
The devices are a block of a 4x4x8 slice.
Arguments:
- hidden: bfloat16 [2048, 2048], P(('dp', 'ep')), parts along dimension 0
- positions: int32 [2048], P(('dp', 'ep')), parts along dimension 0
- expert_ids: int32 [2, 2048, 8], P(None, ('dp', 'ep')), parts along dimension 1
- k_cache: bfloat16 [2, 2048, 16, 4, 128], P(None, ('dp', 'ep')), parts along dimension 1
- v_cache: bfloat16 [2, 2048, 16, 4, 128], P(None, ('dp', 'ep')), parts along dimension 1
- w_query: bfloat16 [2, 2048, 4096], replicated
- w_key: bfloat16 [2, 2048, 512], replicated
- w_value: bfloat16 [2, 2048, 512], replicated
- w_out: bfloat16 [2, 4096, 2048], replicated
- attn_gain: float32 [2, 2048], replicated
- q_gain: float32 [2, 4096], replicated
- k_gain: float32 [2, 512], replicated
- mlp_gain: float32 [2, 2048], replicated
- w_router: bfloat16 [2048, 128], replicated
- w_gate: bfloat16 [128, 2048, 768], P('ep')
- w_up: bfloat16 [128, 2048, 768], P('ep')
- w_down: bfloat16 [128, 768, 2048], P('ep')
Outputs:
- output 1: bfloat16 [2048, 2048], P(('dp', 'ep')), parts along dimension 0
- output 2: bfloat16 [2, 2048, 16, 4, 128], P(None, ('dp', 'ep')), parts along dimension 1
- output 3: bfloat16 [2, 2048, 16, 4, 128], P(None, ('dp', 'ep')), parts along dimension 1
There are 4 independent parts. A program takes and returns all parts, laid end to end along the dimension named above; an argument that names none is the same for every part.
All inputs are finite; a program needn't handle non-finite values.
Results may differ from a plain program's by a relative error of at most 0.02.
Values are sent between devices in bfloat16 or wider.
A program may use at most 768 MiB of HBM per device.

v0:
```python
import jax
import jax.numpy as jnp
from jax import lax
from jax.sharding import PartitionSpec as P

RMS_EPS = 1e-5
ROPE_BASE = 10000.0
CAP_FACTOR = 2


def rms_norm(values, gain_vec):
    values = values.astype(jnp.float32)
    inv_rms = lax.rsqrt(jnp.mean(values * values, axis=-1, keepdims=True) + RMS_EPS)
    return values * inv_rms * gain_vec.astype(jnp.float32)


def rope_rotate(values, positions):
    half_dim = values.shape[-1] // 2
    frequencies = ROPE_BASE ** (-jnp.arange(half_dim, dtype=jnp.float32) / half_dim)
    angles = positions.astype(jnp.float32)[:, None] * frequencies[None, :]
    angles = angles.reshape((angles.shape[0],) + (1,) * (values.ndim - 2) + (half_dim,))
    cosines = jnp.cos(angles)
    sines = jnp.sin(angles)
    first_half = values[..., :half_dim]
    second_half = values[..., half_dim:]
    return jnp.concatenate([first_half * cosines - second_half * sines, second_half * cosines + first_half * sines], axis=-1)


def attention_local(hidden, positions, k_layer, v_layer, w_query, w_key, w_value, w_out, attn_gain, q_gain, k_gain):
    seq_rows = hidden.shape[0]
    cache_len, kv_heads, head_dim = k_layer.shape[1:]
    head_group = w_query.shape[1] // head_dim // kv_heads
    normed = rms_norm(hidden, attn_gain).astype(jnp.bfloat16)
    q_heads = rms_norm(jnp.dot(normed, w_query, preferred_element_type=jnp.float32), q_gain)
    key_row = rms_norm(jnp.dot(normed, w_key, preferred_element_type=jnp.float32), k_gain)
    value_row = jnp.dot(normed, w_value, preferred_element_type=jnp.float32).astype(jnp.bfloat16)
    value_row = value_row.reshape(seq_rows, kv_heads, head_dim)
    q_heads = rope_rotate(q_heads.reshape(seq_rows, kv_heads, head_group, head_dim), positions).astype(jnp.bfloat16)
    key_row = rope_rotate(key_row.reshape(seq_rows, kv_heads, head_dim), positions).astype(jnp.bfloat16)
    score_scale = head_dim ** -0.5
    past_scores = jnp.einsum('bkgd,bskd->bkgs', q_heads, k_layer, preferred_element_type=jnp.float32) * score_scale
    before = (jnp.arange(cache_len)[None, :] < positions[:, None])[:, None, None, :]
    past_scores = jnp.where(before, past_scores, -1e30)
    new_score = jnp.einsum('clhe,cle->clh', q_heads, key_row, preferred_element_type=jnp.float32)[..., None] * score_scale
    peak_score = jnp.maximum(jnp.max(past_scores, axis=-1, keepdims=True), new_score)
    past_exp = jnp.exp(past_scores - peak_score)
    new_exp = jnp.exp(new_score - peak_score)
    prob_sum = jnp.sum(past_exp, axis=-1, keepdims=True) + new_exp
    past_prob = (past_exp / prob_sum).astype(jnp.bfloat16)
    new_prob = (new_exp / prob_sum).astype(jnp.bfloat16)
    mixed_out = jnp.einsum('bkgs,bskd->bkgd', past_prob, v_layer, preferred_element_type=jnp.float32)
    mixed_out = mixed_out + new_prob.astype(jnp.float32) * value_row.astype(jnp.float32)[:, :, None, :]
    mixed_out = mixed_out.astype(jnp.bfloat16).reshape(seq_rows, kv_heads * head_group * head_dim)
    hidden = (hidden.astype(jnp.float32) + jnp.dot(mixed_out, w_out, preferred_element_type=jnp.float32)).astype(jnp.bfloat16)
    return hidden, key_row, value_row


def dispatch_plan(routes, num_experts, capacity):
    seq_rows, top_k = routes.shape
    chosen = jnp.sum(routes[:, :, None] == jnp.arange(num_experts, dtype=jnp.int32)[None, None, :], axis=1, dtype=jnp.int32)
    ranks = jnp.cumsum(chosen, axis=0) - 1
    slot_ids = routes * capacity + jnp.take_along_axis(ranks, routes, axis=1)
    fillers = jnp.repeat(jnp.arange(seq_rows, dtype=jnp.int32), top_k)
    slot_owner = jnp.zeros((num_experts * capacity,), jnp.int32).at[slot_ids.reshape(-1)].set(fillers)
    return slot_ids, slot_owner


def moe_local(hidden, routes, mlp_gain, w_router, w_gate, w_up, w_down, groups):
    seq_rows, model_dim = hidden.shape
    num_experts = w_router.shape[1]
    local_experts = w_gate.shape[0]
    capacity = CAP_FACTOR * seq_rows * routes.shape[1] // num_experts
    normed = rms_norm(hidden, mlp_gain).astype(jnp.bfloat16)
    router_prob = jax.nn.softmax(jnp.dot(normed, w_router, preferred_element_type=jnp.float32), axis=-1)
    gate_vals = jnp.take_along_axis(router_prob, routes, axis=1)
    slot_ids, slot_owner = dispatch_plan(routes, num_experts, capacity)
    send_buf = jnp.take(normed, slot_owner, axis=0).reshape(groups, local_experts, capacity, model_dim)
    recv_buf = lax.all_to_all(send_buf, 'ep', 0, 0, tiled=True)
    gate_act = jnp.einsum('gecd,edf->egcf', recv_buf, w_gate, preferred_element_type=jnp.float32)
    up_act = jnp.einsum('gecd,edf->egcf', recv_buf, w_up, preferred_element_type=jnp.float32)
    act_vals = (jax.nn.silu(gate_act) * up_act).astype(jnp.bfloat16)
    expert_out = jnp.einsum('egcf,efd->gecd', act_vals, w_down, preferred_element_type=jnp.float32).astype(jnp.bfloat16)
    returned = lax.all_to_all(expert_out, 'ep', 0, 0, tiled=True).reshape(num_experts * capacity, model_dim)
    picked = jnp.take(returned, slot_ids, axis=0)
    moe_out = jnp.sum(gate_vals[:, :, None] * picked.astype(jnp.float32), axis=1)
    return (hidden.astype(jnp.float32) + moe_out).astype(jnp.bfloat16)


def solution(mesh):
    groups = mesh.shape['ep']
    batch_axes = ('dp', 'ep')

    def device_step(hidden, positions, expert_ids, k_cache, v_cache, w_query, w_key, w_value, w_out, attn_gain, q_gain, k_gain, mlp_gain, w_router, w_gate, w_up, w_down):
        key_rows = []
        value_rows = []
        for layer_idx in range(expert_ids.shape[0]):
            hidden, key_row, value_row = attention_local(hidden, positions, k_cache[layer_idx], v_cache[layer_idx], w_query[layer_idx], w_key[layer_idx], w_value[layer_idx], w_out[layer_idx], attn_gain[layer_idx], q_gain[layer_idx], k_gain[layer_idx])
            key_rows.append(key_row)
            value_rows.append(value_row)
            hidden = moe_local(hidden, expert_ids[layer_idx], mlp_gain[layer_idx], w_router, w_gate, w_up, w_down, groups)
        hit_mask = (jnp.arange(k_cache.shape[2])[None, :] == positions[:, None])[None, :, :, None, None]
        k_new = jnp.where(hit_mask, jnp.stack(key_rows)[:, :, None], k_cache)
        v_new = jnp.where(hit_mask, jnp.stack(value_rows)[:, :, None], v_cache)
        return hidden, k_new, v_new

    row_spec = P(batch_axes, None)
    cache_spec = P(None, batch_axes, None, None, None)
    full_spec = P()
    expert_spec = P('ep', None, None)
    in_specs = (row_spec, P(batch_axes), P(None, batch_axes, None), cache_spec, cache_spec, full_spec, full_spec, full_spec, full_spec, full_spec, full_spec, full_spec, full_spec, full_spec, expert_spec, expert_spec, expert_spec)
    return jax.shard_map(device_step, mesh=mesh, in_specs=in_specs, out_specs=(row_spec, cache_spec, cache_spec), check_vma=False)
```

profile of v0, /device:TPU:82, one launch (start us, length us, event | category | flops | bytes accessed | tf_op | source)
XLA Modules:
  0.0 467.1 jit_solution(18445349706973391602)
XLA Ops:
  4.7 3.6 gather_fusion.5
  23.0 7.5 %multiply_reduce_fusion.3 = (f32[64]{0:T(128)S(1)}, f32[64,4096]{1,0:T(8,128)S(1)}) fusion(bf16[2,2048,4096]{2,1,0:T(8,128)(2,1)} %param.30, bf16[64,2048]{1,0:T(8,128)(2,1)S(1)} %copy-done.19, f32[2048]{0:T(1024)S(1)} %bitcast.246, f32[64]{0:T(128)S(1)} %add_rsqrt_fusion.7), kind=kOutput, calls=%fused_computation.93 | convolution fusion | flops 1074790400 | bytes 18096640 | tf_op jit(solution)/shard_map/dot_general | solution.py:34
  43.6 7.5 %multiply_reduce_fusion.5 = (f32[64]{0:T(128)S(1)}, f32[64,2048]{1,0:T(8,128)S(1)}) fusion(bf16[2,4096,2048]{2,1,0:T(8,128)(2,1)} %param.33, bf16[8,8,32,128]{3,2,1,0:T(8,128)(2,1)S(1)} %bitcast.252, bf16[64,2048]{1,0:T(8,128)(2,1)S(1)} %copy-done.20), kind=kOutput, calls=%fused_computation.119 | convolution fusion | flops 1074528256 | bytes 18088192 | tf_op jit(solution)/shard_map/dot_general | solution.py:54
  51.3 6.0 %gather_fusion.2 = bf16[1024,2048]{1,0:T(8,128)(2,1)} fusion(bf16[64,2048]{1,0:T(8,128)(2,1)S(1)} %multiply_convert_fusion.3, s32[1024]{0:T(1024)S(1)} %fusion.118), kind=kCustom, calls=%fused_computation.2.clone | custom fusion | bytes 8392704 | tf_op jit(solution)/shard_map/jit(_take)/gather | solution.py:77
  59.9 53.3 %all_to_all.20 = bf16[8,16,8,2048]{3,2,1,0:T(8,128)(2,1)} all-to-all(bf16[8,16,8,2048]{3,2,1,0:T(8,128)(2,1)S(1)} %bitcast.229), channel_id=1, replica_groups=mesh['dp'=4,'ep'=8] {'ep'}, dimensions={0} | all-to-all | bytes 8388608 | tf_op jit(solution)/shard_map/all_to_all | solution.py:78
  113.3 21.6 %fusion.6 = f32[16,8,8,768]{3,2,1,0:T(8,128)} fusion(bf16[16,2048,768]{2,1,0:T(8,128)(2,1)} %param.40, bf16[8,16,8,2048]{3,2,1,0:T(8,128)(2,1)} %all_to_all.20), kind=kOutput, calls=%fused_computation.16 | convolution fusion | flops 3221225472 | bytes 57671680 | tf_op jit(solution)/shard_map/gecd,edf->egcf/dot_general | solution.py:80
  134.8 20.6 %multiply_convert_fusion.1.clone.2 = bf16[16,8,8,768]{3,2,1,0:T(8,128)(2,1)S(1)} fusion(f32[16,8,8,768]{3,2,1,0:T(8,128)} %fusion.6, bf16[16,2048,768]{2,1,0:T(8,128)(2,1)} %param.39, bf16[8,16,8,2048]{3,2,1,0:T(8,128)(2,1)} %all_to_all.20), kind=kOutput, calls=%fused_computation.45.clone.clone.clone | convolution fusion | flops 3225944064 | bytes 59244544 | tf_op jit(solution)/shard_map/gecd,edf->egcf/dot_general | solution.py:79
  155.4 21.0 %convert_bitcast_fusion.1 = bf16[8,16,8,2048]{3,2,0,1:T(8,128)(2,1)} fusion(bf16[16,768,2048]{2,1,0:T(8,128)(2,1)} %param.41, bf16[16,8,8,768]{3,2,1,0:T(8,128)(2,1)S(1)} %multiply_convert_fusion.1.clone.2), kind=kOutput, calls=%fused_computation.37 | convolution fusion | flops 3223322624 | bytes 56098816 | tf_op jit(solution)/shard_map/egcf,efd->gecd/dot_general | solution.py:82
  176.4 4.7 %copy.115 = bf16[8,16,8,2048]{3,2,1,0:T(8,128)(2,1)} copy(bf16[8,16,8,2048]{3,2,0,1:T(8,128)(2,1)} %convert_bitcast_fusion.1) | data formatting | bytes 8388608 | tf_op jit(solution)/shard_map/convert_element_type | solution.py:82
  181.1 5.9 %all-to-all-start.1 = ((bf16[8,16,8,2048]{3,2,1,0:T(8,128)(2,1)}), bf16[8,16,8,2048]{3,2,1,0:T(8,128)(2,1)}, u32[]{:S(2)}, u32[]{:S(2)}) async-start(bf16[8,16,8,2048]{3,2,1,0:T(8,128)(2,1)} %copy.115), calls=%async_computation.1 | async-start | bytes 8388608 | tf_op jit(solution)/shard_map/all_to_all | solution.py:83
  195.8 39.6 %all-to-all-done.1 = bf16[8,16,8,2048]{3,2,1,0:T(8,128)(2,1)} async-done(((bf16[8,16,8,2048]{3,2,1,0:T(8,128)(2,1)}), bf16[8,16,8,2048]{3,2,1,0:T(8,128)(2,1)}, u32[]{:S(2)}, u32[]{:S(2)}) %all-to-all-start.1) | async-done | bytes 4194336 | tf_op jit(solution)/shard_map/all_to_all | solution.py:83
  235.3 7.4 %gather_fusion.3 = bf16[512,2048]{1,0:T(8,128)(2,1)S(1)} fusion(bf16[1024,2048]{1,0:T(8,128)(2,1)} %bitcast.24, s32[1024]{0:T(1024)S(1)} %pad_clamp_fusion.1), kind=kCustom, calls=%fused_computation.3.clone | custom fusion | bytes 4196352 | tf_op jit(solution)/shard_map/jit(_take)/gather | solution.py:84
  245.4 7.7 %multiply_reduce_fusion.2 = (f32[64]{0:T(128)S(1)}, f32[64,4096]{1,0:T(8,128)S(1)}) fusion(bf16[2,2048,4096]{2,1,0:T(8,128)(2,1)} %param.30, bf16[64,2048]{1,0:T(8,128)(2,1)S(1)} %get-tuple-element.10, f32[2048]{0:T(1024)S(1)} %bitcast.243, f32[64]{0:T(128)S(1)} %add_rsqrt_fusion.3), kind=kOutput, calls=%fused_computation.87 | convolution fusion | flops 1074790400 | bytes 18096640 | tf_op jit(solution)/shard_map/dot_general | solution.py:34
  264.3 7.5 %multiply_reduce_fusion.4 = (f32[64]{0:T(128)S(1)}, f32[64,2048]{1,0:T(8,128)S(1)}) fusion(bf16[2,4096,2048]{2,1,0:T(8,128)(2,1)} %param.33, bf16[8,8,32,128]{3,2,1,0:T(8,128)(2,1)S(1)} %bitcast.251, bf16[64,2048]{1,0:T(8,128)(2,1)S(1)} %copy-done.14), kind=kOutput, calls=%fused_computation.114 | convolution fusion | flops 1074528256 | bytes 18088192 | tf_op jit(solution)/shard_map/dot_general | solution.py:54
  272.0 6.4 %gather_fusion.6 = bf16[1024,2048]{1,0:T(8,128)(2,1)} fusion(bf16[64,2048]{1,0:T(8,128)(2,1)S(1)} %multiply_convert_fusion.2, s32[1024]{0:T(1024)S(1)} %fusion.119), kind=kCustom, calls=%fused_computation.6.clone | custom fusion | bytes 8392704 | tf_op jit(solution)/shard_map/jit(_take)/gather | solution.py:77
  281.0 53.0 %all_to_all.21 = bf16[8,16,8,2048]{3,2,1,0:T(8,128)(2,1)} all-to-all(bf16[8,16,8,2048]{3,2,1,0:T(8,128)(2,1)S(1)} %bitcast.230), channel_id=1, replica_groups=mesh['dp'=4,'ep'=8] {'ep'}, dimensions={0} | all-to-all | bytes 8388608 | tf_op jit(solution)/shard_map/all_to_all | solution.py:78
  334.1 21.6 %fusion.4 = f32[16,8,8,768]{3,2,1,0:T(8,128)} fusion(bf16[16,2048,768]{2,1,0:T(8,128)(2,1)} %param.40, bf16[8,16,8,2048]{3,2,1,0:T(8,128)(2,1)} %all_to_all.21), kind=kOutput, calls=%fused_computation.14 | convolution fusion | flops 3221225472 | bytes 57671680 | tf_op jit(solution)/shard_map/gecd,edf->egcf/dot_general | solution.py:80
  355.6 20.6 %multiply_convert_fusion.clone.4 = bf16[16,8,8,768]{3,2,1,0:T(8,128)(2,1)S(1)} fusion(f32[16,8,8,768]{3,2,1,0:T(8,128)} %fusion.4, bf16[16,2048,768]{2,1,0:T(8,128)(2,1)} %param.39, bf16[8,16,8,2048]{3,2,1,0:T(8,128)(2,1)} %all_to_all.21), kind=kOutput, calls=%fused_computation.44.clone.clone.clone.1 | convolution fusion | flops 3225944064 | bytes 59244544 | tf_op jit(solution)/shard_map/gecd,edf->egcf/dot_general | solution.py:79
  376.2 21.0 %convert_bitcast_fusion = bf16[8,16,8,2048]{3,2,0,1:T(8,128)(2,1)} fusion(bf16[16,768,2048]{2,1,0:T(8,128)(2,1)} %param.41, bf16[16,8,8,768]{3,2,1,0:T(8,128)(2,1)S(1)} %multiply_convert_fusion.clone.4), kind=kOutput, calls=%fused_computation.35 | convolution fusion | flops 3223322624 | bytes 56098816 | tf_op jit(solution)/shard_map/egcf,efd->gecd/dot_general | solution.py:82
  397.2 4.7 %copy.134 = bf16[8,16,8,2048]{3,2,1,0:T(8,128)(2,1)} copy(bf16[8,16,8,2048]{3,2,0,1:T(8,128)(2,1)} %convert_bitcast_fusion) | data formatting | bytes 8388608 | tf_op jit(solution)/shard_map/convert_element_type | solution.py:82
  402.0 6.4 %all-to-all-start.3 = ((bf16[8,16,8,2048]{3,2,1,0:T(8,128)(2,1)}), bf16[8,16,8,2048]{3,2,1,0:T(8,128)(2,1)}, u32[]{:S(2)}, u32[]{:S(2)}) async-start(bf16[8,16,8,2048]{3,2,1,0:T(8,128)(2,1)} %copy.134), calls=%async_computation.3 | async-start | bytes 8388608 | tf_op jit(solution)/shard_map/all_to_all | solution.py:83
  416.9 6.1 %broadcast_select_fusion.2 = (bf16[2,64,16,4,128]{4,3,2,1,0:T(4,128)(2,1)}, bf16[2,64,16,4,128]{4,3,2,1,0:T(4,128)(2,1)}) fusion(bf16[2,64,16,4,128]{4,3,2,1,0:T(4,128)(2,1)S(1)} %copy-done.4, pred[64,16]{1,0:T(8,128)(4,1)S(1)} %copy-done.25, bf16[2,64,4,128]{3,2,1,0:T(4,128)(2,1)S(1)} %pad_maximum_fusion.2, bf16[2,64,16,4,128]{4,3,2,1,0:T(4,128)(2,1)} %param.28, ...), kind=kLoop, calls=%fused_computation.66 | loop fusion | flops 2097152 | bytes 8651776 | tf_op jit(solution)/shard_map/jit(_where)/select_n | solution.py:103
  422.9 33.5 %all-to-all-done.3 = bf16[8,16,8,2048]{3,2,1,0:T(8,128)(2,1)} async-done(((bf16[8,16,8,2048]{3,2,1,0:T(8,128)(2,1)}), bf16[8,16,8,2048]{3,2,1,0:T(8,128)(2,1)}, u32[]{:S(2)}, u32[]{:S(2)}) %all-to-all-start.3) | async-done | bytes 4194336 | tf_op jit(solution)/shard_map/all_to_all | solution.py:83
  456.5 7.1 %gather_fusion.7 = bf16[512,2048]{1,0:T(8,128)(2,1)S(1)} fusion(bf16[1024,2048]{1,0:T(8,128)(2,1)} %bitcast.47, s32[1024]{0:T(1024)S(1)} %pad_clamp_fusion), kind=kCustom, calls=%fused_computation.7.clone | custom fusion | bytes 4196352 | tf_op jit(solution)/shard_map/jit(_take)/gather | solution.py:84
  (224 shorter events, 71.0 us)
Async XLA Ops:
  0.6 187.2 %copy-start = (bf16[2048,128]{1,0:T(8,128)(2,1)S(1)}, bf16[2048,128]{1,0:T(8,128)(2,1)}, u32[]{:S(2)}) copy-start(bf16[2048,128]{1,0:T(8,128)(2,1)} %param.38) | copy-start | bytes 1572868
  9.0 8.9 %copy-start.3 = (bf16[2,64,16,4,128]{4,3,2,1,0:T(4,128)(2,1)S(1)}, bf16[2,64,16,4,128]{4,3,2,1,0:T(4,128)(2,1)}, u32[]{:S(2)}) copy-start(bf16[2,64,16,4,128]{4,3,2,1,0:T(4,128)(2,1)} %param.29) | copy-start | bytes 6291460
  23.0 8.0 %copy-start.43 = (f32[64]{0:T(128)}, f32[64]{0:T(128)S(1)}, u32[]{:S(2)}) copy-start(f32[64]{0:T(128)S(1)} %add_rsqrt_fusion.7) | copy-start | bytes 772
  35.4 5.4 %copy-start.30 = (f32[2,2048]{1,0:T(2,128)S(1)}, f32[2,2048]{1,0:T(2,128)}, u32[]{:S(2)}) copy-start(f32[2,2048]{1,0:T(2,128)} %param.37) | copy-start | bytes 49156
  51.3 6.0 %copy-start.35 = (pred[1024]{0:T(1024)(128)(4,1)S(1)}, pred[1024]{0:T(1024)(128)(4,1)}, u32[]{:S(2)}) copy-start(pred[1024]{0:T(1024)(128)(4,1)} %compare_and_fusion.4) | copy-start | bytes 3076
  181.1 54.2 %all-to-all-start.1 = ((bf16[8,16,8,2048]{3,2,1,0:T(8,128)(2,1)}), bf16[8,16,8,2048]{3,2,1,0:T(8,128)(2,1)}, u32[]{:S(2)}, u32[]{:S(2)}) async-start(bf16[8,16,8,2048]{3,2,1,0:T(8,128)(2,1)} %copy.115), calls=%async_computation.1 | async-start | bytes 8388608 | tf_op jit(solution)/shard_map/all_to_all | solution.py:83
  235.3 10.1 %copy-start.33 = (f32[1,2048]{1,0:T(1,128)S(1)}, f32[1,2048]{1,0:T(1,128)}, u32[]{:S(2)}) copy-start(f32[1,2048]{1,0:T(1,128)} %get-tuple-element.33) | copy-start | bytes 24580
  245.4 8.3 %copy-start.13 = (bf16[64,2048]{1,0:T(8,128)(2,1)}, bf16[64,2048]{1,0:T(8,128)(2,1)S(1)}, u32[]{:S(2)}) copy-start(bf16[64,2048]{1,0:T(8,128)(2,1)S(1)} %get-tuple-element.10) | copy-start | bytes 786436
  245.4 7.7 %copy-start.41 = (bf16[2,2048,512]{2,1,0:T(8,128)(2,1)S(1)}, bf16[2,2048,512]{2,1,0:T(8,128)(2,1)}, u32[]{:S(2)}) copy-start(bf16[2,2048,512]{2,1,0:T(8,128)(2,1)} %param.32) | copy-start | bytes 12582916
  245.4 8.3 %copy-start.42 = (bf16[2,2048,512]{2,1,0:T(8,128)(2,1)S(1)}, bf16[2,2048,512]{2,1,0:T(8,128)(2,1)}, u32[]{:S(2)}) copy-start(bf16[2,2048,512]{2,1,0:T(8,128)(2,1)} %param.31) | copy-start | bytes 12582916
  264.3 7.5 %copy-start.27 = (f32[1,2048]{1,0:T(1,128)S(1)}, f32[1,2048]{1,0:T(1,128)}, u32[]{:S(2)}) copy-start(f32[1,2048]{1,0:T(1,128)} %get-tuple-element.31) | copy-start | bytes 24580
  272.0 6.4 %copy-start.34 = (pred[1024]{0:T(1024)(128)(4,1)S(1)}, pred[1024]{0:T(1024)(128)(4,1)}, u32[]{:S(2)}) copy-start(pred[1024]{0:T(1024)(128)(4,1)} %compare_and_fusion.1) | copy-start | bytes 3076
  401.9 6.4 %copy-start.16 = (bf16[64,512]{1,0:T(8,128)(2,1)S(1)}, bf16[64,512]{1,0:T(8,128)(2,1)}, u32[]{:S(2)}) copy-start(bf16[64,512]{1,0:T(8,128)(2,1)} %copy-done.15) | copy-start | bytes 196612
  401.9 7.0 %copy-start.31 = (s32[64,8]{0,1:T(8,128)S(1)}, s32[64,8]{0,1:T(8,128)}, u32[]{:S(2)}) copy-start(s32[64,8]{0,1:T(8,128)} %get-tuple-element.69) | copy-start | bytes 6148
  401.9 7.2 %copy-start.37 = (pred[64,8]{0,1:T(8,128)(4,1)S(1)}, pred[64,8]{0,1:T(8,128)(4,1)}, u32[]{:S(2)}) copy-start(pred[64,8]{0,1:T(8,128)(4,1)} %get-tuple-element.6) | copy-start | bytes 1540
  401.9 7.9 %copy-start.18 = (bf16[64,512]{1,0:T(8,128)(2,1)S(1)}, bf16[64,512]{1,0:T(8,128)(2,1)}, u32[]{:S(2)}) copy-start(bf16[64,512]{1,0:T(8,128)(2,1)} %copy-done.17) | copy-start | bytes 196612
  402.0 9.2 %copy-start.2 = (s32[512]{0:T(512)S(1)}, s32[512]{0:T(512)}, u32[]{:S(2)}) copy-start(s32[512]{0:T(512)} %copy-done.1) | copy-start | bytes 6148
  402.0 54.5 %all-to-all-start.3 = ((bf16[8,16,8,2048]{3,2,1,0:T(8,128)(2,1)}), bf16[8,16,8,2048]{3,2,1,0:T(8,128)(2,1)}, u32[]{:S(2)}, u32[]{:S(2)}) async-start(bf16[8,16,8,2048]{3,2,1,0:T(8,128)(2,1)} %copy.134), calls=%async_computation.3 | async-start | bytes 8388608 | tf_op jit(solution)/shard_map/all_to_all | solution.py:83
  411.2 5.5 %copy-start.10 = (bf16[64,4,64]{2,1,0:T(4,128)(2,1)S(1)}, bf16[64,4,64]{2,1,0:T(4,128)(2,1)}, u32[]{:S(2)}) copy-start(bf16[64,4,64]{2,1,0:T(4,128)(2,1)} %copy-done.9) | copy-start | bytes 98308
  411.2 5.5 %copy-start.12 = (bf16[64,4,64]{2,1,0:T(4,128)(2,1)S(1)}, bf16[64,4,64]{2,1,0:T(4,128)(2,1)}, u32[]{:S(2)}) copy-start(bf16[64,4,64]{2,1,0:T(4,128)(2,1)} %copy-done.11) | copy-start | bytes 98308
  411.2 5.7 %copy-start.4 = (bf16[2,64,16,4,128]{4,3,2,1,0:T(4,128)(2,1)S(1)}, bf16[2,64,16,4,128]{4,3,2,1,0:T(4,128)(2,1)}, u32[]{:S(2)}) copy-start(bf16[2,64,16,4,128]{4,3,2,1,0:T(4,128)(2,1)} %param.29) | copy-start | bytes 6291460
  411.2 5.7 %copy-start.25 = (pred[64,16]{1,0:T(8,128)(4,1)S(1)}, pred[64,16]{1,0:T(8,128)(4,1)}, u32[]{:S(2)}) copy-start(pred[64,16]{1,0:T(8,128)(4,1)} %get-tuple-element.47) | copy-start | bytes 3076
  456.5 7.2 %copy-start.24 = (f32[64,8]{1,0:T(8,128)S(1)}, f32[64,8]{1,0:T(8,128)}, u32[]{:S(2)}) copy-start(f32[64,8]{1,0:T(8,128)} %copy.126) | copy-start | bytes 6148
  456.5 7.2 %copy-start.26 = (pred[64,8]{1,0:T(8,128)(4,1)S(1)}, pred[64,8]{1,0:T(8,128)(4,1)}, u32[]{:S(2)}) copy-start(pred[64,8]{1,0:T(8,128)(4,1)} %copy.130) | copy-start | bytes 1540
  (23 other events, 73.8 us)
where the time goes:
time: 472 us; the launch traced here: 467 us
  matrix products  170 us (36%)
  blocking collectives  106 us (22%)
  local copies, waits for them, and re-layouts  73.4 us (16%)
  waiting for transfers between devices  73.1 us (15%)
  other arithmetic  29.8 us (6%)
  starting transfers between devices  12.2 us (3%)
    all_to_all x2, blocking collectives, moe_local(): recv_buf = lax.all_to_all(send_buf, 'ep', 0, 0, tiled=True)  106 us
    all_to_all x2, waiting for transfers between devices, moe_local(): lax.all_to_all(expert_out, 'ep', 0, 0, tiled=True)  73.1 us
    dot_general x2, matrix products, moe_local(): jnp.einsum('gecd,edf->egcf', recv_buf, w_up, preferred_element_type=jnp.f...  43.1 us
    dot_general x2, matrix products, moe_local(): jnp.einsum('egcf,efd->gecd', act_vals, w_down, preferred_element_type=jnp...  42.1 us
    dot_general x2, matrix products, moe_local(): jnp.einsum('gecd,edf->egcf', recv_buf, w_gate, preferred_element_type=jnp...  41.1 us
    dot_general x2, matrix products, attention_local(): jnp.dot(normed, w_query, preferred_element_type=jnp.float32)  15.2 us
    dot_general x2, matrix products, attention_local(): jnp.dot(mixed_out, w_out, preferred_element_type=jnp.float32)  15 us
    gather x2, local copies, waits for them, and re-layouts, moe_local(): picked = jnp.take(returned, slot_ids, axis=0)  14.5 us
  transfers between devices with their start and end apart: 2, of which 2 were waited for; matrix products, arithmetic and copies ran while one was open for 5% of the time, Pallas kernels for 0%

commit v1 on v0

v1 whole, which is shorter than its diff:
```python
import functools

import jax
import jax.numpy as jnp
import numpy as np
from jax import lax
from jax.experimental import pallas as pl
from jax.experimental.pallas import tpu as pltpu
from jax.sharding import PartitionSpec as P

MESH = pl.DeviceIdType.MESH
F32 = jnp.float32
BF16 = jnp.bfloat16
RMS_EPS = 1e-5
ROPE_BASE = 10000.0
CB = 512
SLOTS = 15


def rms_scale(v):
    return lax.rsqrt(jnp.mean(v * v, axis=-1, keepdims=True) + RMS_EPS)


def dot(a, b):
    return jnp.dot(a, b, preferred_element_type=F32)


def dot_t0(a, b):
    return lax.dot_general(a, b, (((0,), (0,)), ((), ())), preferred_element_type=F32)


def step_kernel(dims, hid, pos, ids, kc, vc, wq, wk, wv, wo, ag, qg, kg, mg, wr, wg, wu, wd, ctab, stab,
                out, kn, vn,
                ring, rsem, ssem, posv, idsv, agv, qgv, kgv, mgv, ctv, stv, xcur, hbuf, qf, kf, vf, mx,
                kcv, vcv, posb, cosb, sinb, rk, xg, xd, act, yb, cb, part, prt, far, comb, near, wrv, knb, vnb,
                rkss, rkrs, agss, agrs, rsss, rsrs, osem):
    n_layers, n_ep, T, D, QW, KVW, HD, S, E, EL, F, CAP = dims
    KV = KVW // HD
    H = QW // HD
    HG = H // KV
    NX = n_ep // 2
    NCH = D // CB
    NQ = QW // CB
    NO = NCH * (QW // D)
    NGU = 3 * EL
    ND1 = EL * F // D
    ND = NCH * ND1
    O_AT = NQ + 2
    G_AT = O_AT + NO
    D_AT = G_AT + NGU
    TOT = D_AT + ND
    CF = F - CB

    me = lax.axis_index("ep")
    core = lax.rem(me, 2)
    chip = me // 2
    sgn = 1 - 2 * core
    nchip = lax.rem(chip + sgn + NX, NX)
    pchip = lax.rem(chip - sgn + NX, NX)
    ochip = lax.rem(chip + 2, NX)
    partner = me + sgn
    nxt = nchip * 2 + core
    prv = pchip * 2 + core
    opp = ochip * 2 + core

    def slot_rows(k):
        return pl.ds(pl.multiple_of(lax.rem(k, SLOTS) * D, D), D)

    def issue(k):
        @pl.when(k < n_layers * TOT)
        def _():
            l = k // TOT
            r = lax.rem(k, TOT)
            s = lax.rem(k, SLOTS)
            dst = ring.at[slot_rows(k)]
            sem = rsem.at[s]

            def cols(i):
                return pl.ds(pl.multiple_of(i * CB, CB), CB)

            @pl.when(r < NQ)
            def _():
                pltpu.make_async_copy(wq.at[l, :, cols(r)], dst, sem).start()

            @pl.when(r == NQ)
            def _():
                pltpu.make_async_copy(wk.at[l], dst, sem).start()

            @pl.when(r == NQ + 1)
            def _():
                pltpu.make_async_copy(wv.at[l], dst, sem).start()

            @pl.when((r >= O_AT) & (r < G_AT))
            def _():
                j = r - O_AT
                half = lax.rem(j, QW // D)
                rows = pl.ds(pl.multiple_of(half * D, D), D)
                pltpu.make_async_copy(wo.at[l, rows, cols(j // (QW // D))], dst, sem).start()

            @pl.when((r >= G_AT) & (r < D_AT))
            def _():
                j = r - G_AT
                e = j // 3
                piece = lax.rem(j, 3)

                @pl.when(piece == 0)
                def _():
                    pltpu.make_async_copy(wg.at[e, :, 0:CB], dst, sem).start()

                @pl.when(piece == 1)
                def _():
                    pltpu.make_async_copy(wu.at[e, :, 0:CB], dst, sem).start()

                @pl.when(piece == 2)
                def _():
                    pltpu.make_async_copy(wg.at[e, :, CB:F], ring.at[slot_rows(k), 0:CF], sem).start()
                    pltpu.make_async_copy(wu.at[e, :, CB:F], ring.at[slot_rows(k), CF:CB], sem).start()

            @pl.when(r >= D_AT)
            def _():
                j = r - D_AT
                rows = pl.ds(pl.multiple_of(lax.rem(j, ND1) * D, D), D)
                pltpu.make_async_copy(wd.at[rows, cols(j // ND1)], dst, sem).start()

    def arrive(k):
        pltpu.make_async_copy(wk.at[0], ring.at[slot_rows(k)], rsem.at[lax.rem(k, SLOTS)]).wait()

    smalls = ((hid, xcur), (pos, posv), (ids, idsv), (ag, agv), (qg, qgv), (kg, kgv), (mg, mgv), (ctab, ctv), (stab, stv))
    small_copies = [pltpu.make_async_copy(a, b, ssem.at[i]) for i, (a, b) in enumerate(smalls)]
    for cp in small_copies:
        cp.start()

    def prime(k, carry):
        issue(k)
        return carry

    lax.fori_loop(0, SLOTS, prime, 0)
    big_copies = [pltpu.make_async_copy(a, b, ssem.at[len(smalls) + i]) for i, (a, b) in enumerate(((kc, kcv), (vc, vcv), (wr, wrv)))]
    for cp in big_copies:
        cp.start()

    barrier = pltpu.get_barrier_semaphore()
    for dev in (partner, nxt, prv):
        pl.semaphore_signal(barrier, inc=1, device_id={"ep": dev}, device_id_type=MESH)
    for cp in small_copies:
        cp.wait()

    posf = jnp.broadcast_to(posv[...].astype(F32), (T, HD))
    posb[...] = posf
    cos = jnp.zeros((T, HD), F32)
    sin = jnp.zeros((T, HD), F32)
    for s in range(S):
        hit = posf == float(s)
        cos = jnp.where(hit, ctv[s:s + 1, :], cos)
        sin = jnp.where(hit, stv[s:s + 1, :], sin)
    cosb[...] = cos
    sinb[...] = sin

    lane_e = lax.broadcasted_iota(jnp.int32, (T, E), 1)
    tril = (lax.broadcasted_iota(jnp.int32, (T, T), 0) > lax.broadcasted_iota(jnp.int32, (T, T), 1))
    tril = jnp.where(tril, 1.0, 0.0).astype(BF16)
    for l in range(n_layers):
        idl = idsv[l]
        chosen = jnp.zeros((T, E), F32)
        for j in range(idl.shape[1]):
            chosen = jnp.where(idl[:, j:j + 1] == lane_e, 1.0, chosen)
        rank = dot(tril, chosen.astype(BF16))
        rk[me, :, l * E:(l + 1) * E] = jnp.where(chosen > 0.5, rank, -1.0).astype(BF16)

    pl.semaphore_wait(barrier, 3)

    def rcopy(src, dst, ss, rs, dev):
        return pltpu.make_async_remote_copy(src_ref=src, dst_ref=dst, send_sem=ss, recv_sem=rs, device_id={"ep": dev}, device_id_type=MESH)

    def gather_stages(view, ss, rs):
        def cp(block, kind, dev):
            return rcopy(view(block), view(block), ss(kind), rs(kind), dev)

        def own():
            cp(me, 0, partner).start()
            cp(me, 1, nxt).start()
            cp(me, 2, prv).start()

        def forward():
            cp(prv, 1, nxt).wait_recv()
            cp(prv, 3, nxt).start()
            cp(prv, 4, partner).start()
            cp(nxt, 2, prv).wait_recv()
            cp(nxt, 5, partner).start()

        def across():
            cp(opp, 3, nxt).wait_recv()
            cp(opp, 6, partner).start()

        def finish():
            for kind in (0, 4, 5, 6):
                cp(me, kind, partner).wait_recv()
            for kind in range(7):
                cp(me, kind, partner).wait_send()

        return own, forward, across, finish

    own, forward, across, finish = gather_stages(lambda b: rk.at[b], lambda i: rkss.at[i], lambda i: rkrs.at[i])
    own()
    forward()
    across()
    finish()

    for cp in big_copies:
        cp.wait()

    col = lax.broadcasted_iota(jnp.int32, (8, S * KV * 8), 1)
    col_b = col // (S * KV)
    col_s = lax.rem(col // KV, S).astype(F32)
    col_kv = lax.rem(col, KV)
    diag = col_b == lax.broadcasted_iota(jnp.int32, (8, S * KV * 8), 0)
    GR = 8 * S * KV

    def layer(l, carry):
        base = l * TOT
        x = xcur[...].astype(F32)
        hbuf[...] = (x * rms_scale(x) * agv[pl.ds(l, 1), :]).astype(BF16)

        def q_step(j, c):
            k = base + j
            arrive(k)
            qf[:, pl.ds(pl.multiple_of(j * CB, CB), CB)] = dot(hbuf[...], ring[slot_rows(k), :])
            issue(k + SLOTS)
            return c

        lax.fori_loop(0, NQ, q_step, 0)
        arrive(base + NQ)
        kf[...] = dot(hbuf[...], ring[slot_rows(base + NQ), :])
        issue(base + NQ + SLOTS)
        arrive(base + NQ + 1)
        vf[...] = dot(hbuf[...], ring[slot_rows(base + NQ + 1), :])
        issue(base + NQ + 1 + SLOTS)

        def attend(g, c):
            rows = pl.ds(pl.multiple_of(g * 8, 8), 8)
            crows = pl.ds(pl.multiple_of(g * GR, GR), GR)
            cos8 = cosb[rows, :]
            sin8 = sinb[rows, :]
            pos8 = posb[rows, :]

            def rope(t):
                return t * cos8 + pltpu.roll(t, HD // 2, 1) * sin8

            q8 = qf[rows, :]
            q8 = q8 * rms_scale(q8) * qgv[pl.ds(l, 1), :]
            qs = jnp.concatenate([rope(q8[:, h * HD:(h + 1) * HD]) for h in range(H)], axis=0).astype(BF16)
            k8 = kf[rows, :]
            k8 = k8 * rms_scale(k8) * kgv[pl.ds(l, 1), :]
            k_tiles = [rope(k8[:, h * HD:(h + 1) * HD]) for h in range(KV)]
            kf[rows, :] = jnp.concatenate(k_tiles, axis=1)
            v8 = vf[rows, :]
            v_tiles = [v8[:, h * HD:(h + 1) * HD] for h in range(KV)]
            fresh = jnp.concatenate([jnp.concatenate(k_tiles, axis=0), jnp.concatenate(v_tiles, axis=0), jnp.ones((8 * KV, HD), F32)], axis=1).astype(BF16)
            posw = jnp.concatenate([pos8] * (GR // HD), axis=1)
            hit8 = diag & (col_s == posw)
            ok8 = diag & (col_s <= posw)
            place = jnp.concatenate([jnp.where(hit8 & (col_kv == h), 1.0, 0.0) for h in range(KV)], axis=0).astype(BF16)
            okay = jnp.concatenate([jnp.where(ok8 & (col_kv == h), 1.0, 0.0)[None, None] for h in range(KV)], axis=0)
            put = dot_t0(place, fresh)
            hits = put[:, 2 * HD:] > 0.5
            kb = jnp.where(hits, put[:, :HD], kcv[l, crows, :].astype(F32)).astype(BF16)
            vb = jnp.where(hits, put[:, HD:2 * HD], vcv[l, crows, :].astype(F32)).astype(BF16)
            sc = lax.dot_general(qs, kb, (((1,), (1,)), ((), ())), preferred_element_type=F32) * (HD ** -0.5)
            sc = sc.reshape(KV, HG, 8, GR)
            sc = jnp.where(jnp.broadcast_to(okay, sc.shape) > 0.5, sc, -1e30).reshape(H * 8, GR)
            ex = jnp.exp(sc - jnp.max(sc, axis=-1, keepdims=True))
            pr = (ex * (1.0 / jnp.sum(ex, axis=-1, keepdims=True))).astype(BF16)
            mixed = dot(pr, vb)
            qf[rows, :] = jnp.concatenate([mixed[h * 8:(h + 1) * 8, :] for h in range(H)], axis=1)
            return c

        lax.fori_loop(0, T // 8, attend, 0)
        mx[...] = qf[...].astype(BF16)

        @pl.when(l > 0)
        def _():
            pltpu.make_async_copy(knb, kn.at[0], osem.at[0]).wait()
            pltpu.make_async_copy(vnb, vn.at[0], osem.at[1]).wait()

        knb[...] = kf[...].astype(BF16)
        vnb[...] = vf[...].astype(BF16)
        pltpu.make_async_copy(knb, kn.at[l], osem.at[0]).start()
        pltpu.make_async_copy(vnb, vn.at[l], osem.at[1]).start()

        stages = []
        for n in range(NCH):
            cs = slice(n * CB, (n + 1) * CB)
            stages.append(gather_stages(lambda b, cs=cs: xg.at[b, :, cs], lambda i, n=n: agss.at[n, i], lambda i, n=n: agrs.at[n, i]))
        for n in range(NCH):
            cs = slice(n * CB, (n + 1) * CB)
            acc = xcur[:, cs].astype(F32)
            total = None
            for half in range(QW // D):
                k = base + O_AT + n * (QW // D) + half
                arrive(k)
                term = dot(mx[:, half * D:(half + 1) * D], ring[slot_rows(k), :])
                total = term if total is None else total + term
                issue(k + SLOTS)
            xn = (acc + total).astype(BF16)
            xcur[:, cs] = xn
            xg[me, :, cs] = xn
            stages[n][0]()
            if n >= 1:
                stages[n - 1][1]()
            if n >= 2:
                stages[n - 2][2]()
        stages[NCH - 1][1]()
        stages[NCH - 2][2]()
        stages[NCH - 1][2]()
        for n in range(NCH):
            stages[n][3]()

        lane = lax.broadcasted_iota(jnp.int32, (E, EL * 2 * CAP), 1)
        expand = jnp.where(lax.broadcasted_iota(jnp.int32, (E, EL * 2 * CAP), 0) == me * EL + lane // (2 * CAP), 1.0, 0.0).astype(BF16)
        lane_t = lax.broadcasted_iota(jnp.int32, (2 * T, EL * 2 * CAP), 1)
        same = lax.rem(lane_t // CAP, 2) == lax.broadcasted_iota(jnp.int32, (2 * T, EL * 2 * CAP), 0) // T
        lane_c = lax.rem(lane_t, CAP).astype(F32)
        lcol = pl.ds(pl.multiple_of(l * E, E), E)

        def route(xc, c):
            xp = xg[pl.ds(xc * 2, 2)].reshape(2 * T, D).astype(F32)
            hp = (xp * rms_scale(xp) * mgv[pl.ds(l, 1), :]).astype(BF16)
            logits = dot(hp, wrv[...])
            ex = jnp.exp(logits - jnp.max(logits, axis=-1, keepdims=True))
            prob = ex * (1.0 / jnp.sum(ex, axis=-1, keepdims=True))
            ranks = dot(rk[pl.ds(xc * 2, 2), :, lcol].reshape(2 * T, E), expand)
            pick = same & (ranks == lane_c)
            g1 = prob.astype(BF16)
            r1 = prob - g1.astype(F32)
            g2 = r1.astype(BF16)
            g3 = (r1 - g2.astype(F32)).astype(BF16)
            for i, gpart in enumerate((g1, g2, g3)):
                cb[xc, i * 2 * T:(i + 1) * 2 * T, :] = jnp.where(pick, dot(gpart, expand), 0.0).astype(BF16)
            onehot = jnp.where(pick, 1.0, 0.0).astype(BF16)
            for n in range(NCH):
                rows = dot_t0(onehot, hp[:, n * CB:(n + 1) * CB]).astype(BF16)
                xd[:, pl.ds(pl.multiple_of(xc * 2 * CAP, 2 * CAP), 2 * CAP), n * CB:(n + 1) * CB] = rows.reshape(EL, 2 * CAP, CB)
            return c

        lax.fori_loop(0, NX, route, 0)

        def gate_up(e, c):
            k = base + G_AT + 3 * e
            xe = xd[e]
            arrive(k)
            ga = dot(xe, ring[slot_rows(k), :])
            issue(k + SLOTS)
            arrive(k + 1)
            up = dot(xe, ring[slot_rows(k + 1), :])
            issue(k + 1 + SLOTS)
            act[e, :, 0:CB] = (jax.nn.silu(ga) * up).astype(BF16)
            arrive(k + 2)
            gu = dot(xe, ring[slot_rows(k + 2), :])
            issue(k + 2 + SLOTS)
            act[e, :, CB:F] = (jax.nn.silu(gu[:, :CF]) * gu[:, CF:]).astype(BF16)
            return c

        lax.fori_loop(0, EL, gate_up, 0)

        def send0(n):
            return rcopy(part.at[n, 1 - core], prt.at[n], rsss.at[n, 0], rsrs.at[n, 0], partner)

        def send_far(n):
            return rcopy(part.at[n, core, ochip], far.at[n], rsss.at[n, 1], rsrs.at[n, 1], nxt)

        def send_near(n):
            return rcopy(part.at[n, core, pchip], near.at[n], rsss.at[n, 2], rsrs.at[n, 2], prv)

        def send_comb(n):
            return rcopy(part.at[n, core, nchip], comb.at[n], rsss.at[n, 3], rsrs.at[n, 3], nxt)

        def stage1(n):
            send0(n).wait_recv()
            part[n, core] = part[n, core] + prt[n]
            send_far(n).start()
            send_near(n).start()

        def stage2(n):
            send_far(n).wait_recv()
            part[n, core, nchip] = part[n, core, nchip] + far[n]
            send_comb(n).start()

        def stage3(n):
            send_near(n).wait_recv()
            send_comb(n).wait_recv()
            cs = pl.ds(pl.multiple_of(n * CB, CB), CB)
            total = part[n, core, chip] + comb[n] + near[n]
            xcur[:, cs] = (xcur[:, cs].astype(F32) + total).astype(BF16)

        def down(n, c):
            def piece(i, cc):
                k = base + D_AT + n * ND1 + 3 * i
                for j in range(3):
                    arrive(k + j)
                row0 = lax.rem(k, SLOTS) * D
                per = 3 * D // F
                for m in range(per):
                    e = i * per + m
                    wrows = pl.ds(pl.multiple_of(row0 + m * F, 256), F)
                    y = dot(act[e], ring[wrows, :]).astype(BF16)
                    for xc in range(NX):
                        yb[xc, pl.ds(pl.multiple_of(e * 2 * CAP, 2 * CAP), 2 * CAP), :] = y[xc * 2 * CAP:(xc + 1) * 2 * CAP, :]
                for j in range(3):
                    issue(k + j + SLOTS)
                return cc

            lax.fori_loop(0, ND1 // 3, piece, 0)
            for xc in range(NX):
                p3 = dot(cb[xc], yb[xc])
                p1 = p3[:2 * T] + (p3[2 * T:4 * T] + p3[4 * T:])
                part[n, 0, xc] = p1[:T]
                part[n, 1, xc] = p1[T:]
            send0(n).start()

            @pl.when(n >= 1)
            def _():
                stage1(n - 1)

            @pl.when(n >= 2)
            def _():
                stage2(n - 2)

            @pl.when(n >= 3)
            def _():
                stage3(n - 3)

            return c

        lax.fori_loop(0, NCH, down, 0)
        stage1(NCH - 1)
        stage2(NCH - 2)
        stage3(NCH - 3)
        stage2(NCH - 1)
        stage3(NCH - 2)
        stage3(NCH - 1)

        def drain(n, c):
            send0(n).wait_send()
            send_far(n).wait_send()
            send_near(n).wait_send()
            send_comb(n).wait_send()
            return c

        lax.fori_loop(0, NCH, drain, 0)
        return carry

    lax.fori_loop(0, n_layers, layer, 0)
    last = pltpu.make_async_copy(xcur, out, osem.at[2])
    last.start()
    pltpu.make_async_copy(knb, kn.at[0], osem.at[0]).wait()
    pltpu.make_async_copy(vnb, vn.at[0], osem.at[1]).wait()
    last.wait()


def rope_tables(cache_len, head_dim):
    half = head_dim // 2
    freq = np.float32(ROPE_BASE) ** (-np.arange(half, dtype=np.float32) / np.float32(half))
    ang = np.arange(cache_len, dtype=np.float32)[:, None] * freq.astype(np.float32)[None, :]
    cos = np.cos(ang).astype(np.float32)
    sin = np.sin(ang).astype(np.float32)
    return np.concatenate([cos, cos], axis=1), np.concatenate([-sin, sin], axis=1)


def solution(mesh):
    n_ep = mesh.shape['ep']
    batch_axes = ('dp', 'ep')

    def device_step(hidden, positions, expert_ids, k_cache, v_cache, w_query, w_key, w_value, w_out, attn_gain, q_gain, k_gain, mlp_gain, w_router, w_gate, w_up, w_down):
        L, T, top_k = expert_ids.shape
        D = hidden.shape[1]
        S, KV, HD = k_cache.shape[2:]
        QW = w_query.shape[2]
        KVW = w_key.shape[2]
        E = w_router.shape[1]
        EL, _, F = w_gate.shape
        CAP = 2 * T * top_k // E
        NX = n_ep // 2
        NCH = D // CB
        dims = (L, n_ep, T, D, QW, KVW, HD, S, E, EL, F, CAP)
        ctab, stab = rope_tables(S, HD)
        rows = T * S * KV
        anyspec = pl.BlockSpec(memory_space=pl.ANY)
        V = pltpu.VMEM
        DMA = pltpu.SemaphoreType.DMA
        scratch = [
            V((SLOTS * D, CB), BF16), DMA((SLOTS,)), DMA((12,)),
            V((T, 1), jnp.int32), V((L, T, top_k), jnp.int32),
            V((L, D), F32), V((L, QW), F32), V((L, KVW), F32), V((L, D), F32),
            V((S, HD), F32), V((S, HD), F32),
            V((T, D), BF16), V((T, D), BF16), V((T, QW), F32), V((T, KVW), F32), V((T, KVW), F32), V((T, QW), BF16),
            V((L, rows, HD), BF16), V((L, rows, HD), BF16),
            V((T, HD), F32), V((T, HD), F32), V((T, HD), F32),
            V((n_ep, T, L * E), BF16), V((n_ep, T, D), BF16),
            V((EL, n_ep * CAP, D), BF16), V((EL, n_ep * CAP, F), BF16),
            V((NX, EL * 2 * CAP, CB), BF16), V((NX, 6 * T, EL * 2 * CAP), BF16),
            V((NCH, 2, NX, T, CB), F32), V((NCH, NX, T, CB), F32),
            V((NCH, T, CB), F32), V((NCH, T, CB), F32), V((NCH, T, CB), F32),
            V((D, E), BF16), V((T, KVW), BF16), V((T, KVW), BF16),
            DMA((7,)), DMA((7,)), DMA((NCH, 7)), DMA((NCH, 7)), DMA((NCH, 4)), DMA((NCH, 4)), DMA((3,)),
        ]
        out, kn, vn = pl.pallas_call(
            functools.partial(step_kernel, dims),
            out_shape=(jax.ShapeDtypeStruct((T, D), BF16), jax.ShapeDtypeStruct((L, T, KVW), BF16), jax.ShapeDtypeStruct((L, T, KVW), BF16)),
            in_specs=[anyspec] * 19,
            out_specs=(anyspec,) * 3,
            scratch_shapes=scratch,
            compiler_params=pltpu.CompilerParams(collective_id=0, has_side_effects=True, vmem_limit_bytes=67043328),
            name="moe_decode",
        )(hidden, positions.reshape(T, 1), expert_ids, k_cache.reshape(L, rows, HD), v_cache.reshape(L, rows, HD),
          w_query, w_key, w_value, w_out, attn_gain, q_gain, k_gain, mlp_gain, w_router, w_gate, w_up,
          w_down.reshape(EL * F, D), jnp.asarray(ctab), jnp.asarray(stab))
        hit = (jnp.arange(S)[None, :] == positions[:, None])[None, :, :, None, None]
        k_new = jnp.where(hit, kn.reshape(L, T, 1, KV, HD), k_cache)
        v_new = jnp.where(hit, vn.reshape(L, T, 1, KV, HD), v_cache)
        return out, k_new, v_new

    row_spec = P(batch_axes, None)
    cache_spec = P(None, batch_axes, None, None, None)
    full_spec = P()
    expert_spec = P('ep', None, None)
    in_specs = (row_spec, P(batch_axes), P(None, batch_axes, None), cache_spec, cache_spec, full_spec, full_spec, full_spec, full_spec, full_spec, full_spec, full_spec, full_spec, full_spec, expert_spec, expert_spec, expert_spec)
    return jax.shard_map(device_step, mesh=mesh, in_specs=in_specs, out_specs=(row_spec, cache_spec, cache_spec), check_vma=False)
```

time: 472 us -> 204 us (0.43)
  Pallas kernels: 0 us -> 190 us
  matrix products: 170 us -> 0 us
  blocking collectives: 106 us -> 0 us
  waiting for transfers between devices: 73.1 us -> 0 us
  local copies, waits for them, and re-layouts: 73.4 us -> 5.37 us
  other arithmetic: 29.8 us -> 7.86 us
  starting transfers between devices: 12.2 us -> 0 us
    pallas_call x0 -> x1, Pallas kernels: none -> 190 us  [device_step(): pl.pallas_call(functools.partial(step_kernel, dims), out_shape=(jax.Shape...]
    dot_general x22 -> x0, matrix products: 170 us -> none  [the longest x2 43.1 us: moe_local(): jnp.einsum('gecd,edf->egcf', recv_buf, w_up, preferred_element_type=jnp.f...]
    all_to_all x2 -> x0, blocking collectives: 106 us -> none  [moe_local(): recv_buf = lax.all_to_all(send_buf, 'ep', 0, 0, tiled=True)]
    all_to_all x2 -> x0, waiting for transfers between devices: 73.1 us -> none  [moe_local(): lax.all_to_all(expert_out, 'ep', 0, 0, tiled=True)]
    gather x20 -> x0, local copies, waits for them, and re-layouts: 42.4 us -> none  [the longest x2 14.5 us: moe_local(): picked = jnp.take(returned, slot_ids, axis=0)]
    all_to_all x2 -> x0, starting transfers between devices: 12.2 us -> none  [moe_local(): lax.all_to_all(expert_out, 'ep', 0, 0, tiled=True)]
    convert_element_type x6 -> x0, local copies, waits for them, and re-layouts: 10.4 us -> none  [the longest x2 9.44 us: moe_local(): jnp.einsum('egcf,efd->gecd', act_vals, w_down, preferred_element_type=jnp...]
    reduce_sum x10 -> x0, other arithmetic: 7.55 us -> none  [the longest x2 5.04 us: moe_local(): jnp.sum(gate_vals[:, :, None] * picked.astype(jnp.float32), axis=1)]
  transfers between devices with their start and end apart: 2 -> 0, of which waited for: 2 -> 0; matrix products, arithmetic and copies ran while one was open for 5% -> 0% of each run, Pallas kernels for 0% -> 0%
where the time goes in v1:
time: 204 us; the launch traced here: 203 us
  Pallas kernels  190 us (93%)
  other arithmetic  7.86 us (4%)
  local copies, waits for them, and re-layouts  5.37 us (3%)
    pallas_call x1, Pallas kernels, device_step(): pl.pallas_call(functools.partial(step_kernel, dims), out_shape=(jax.Shape...  190 us
    select_n x1, other arithmetic, device_step(): v_new = jnp.where(hit, vn.reshape(L, T, 1, KV, HD), v_cache)  6.54 us

profile of v1, /device:TPU:82, one launch (start us, length us, event | category | flops | bytes accessed | tf_op | source)
XLA Modules:
  0.0 203.4 jit_solution(14306125810010083244)
XLA Ops:
  0.6 1.3 iota_compare_fusion
  2.0 1.4 copy.22.pos
  3.3 1.4 copy.23.ids
  4.7 189.5 %moe_decode.1 = (bf16[64,2048]{1,0:T(8,128)(2,1)}, bf16[2,64,512]{2,1,0:T(8,128)(2,1)}, bf16[2,64,512]{2,1,0:T(8,128)(2,1)}) custom-call(bf16[64,2048]{1,0:T(8,128)(2,1)} %hid.1, s32[64,1]{1,0:T(8,128)} %copy.22.pos, s32[2,64,8]{2,1,0:T(8,128)} %copy.23.ids, bf16[2,4096,128]{2,1,0:T(8,128)(2,1)} %bitcast.5, bf16[2,4096,128]{2,1,0:T(8,128)(2,1)} %bitcast.6, ...), custom_call_target="tpu_custom_call" | custom-call | tf_op jit(solution)/shard_map/moe_decode/pallas_call | solution.py:506
  194.3 0.9 broadcast_in_dim.32
  195.2 0.9 broadcast_in_dim.34
  196.2 0.0 copy-start
  196.2 6.5 %broadcast_select_fusion = (bf16[2,64,16,4,128]{4,3,2,1,0:T(4,128)(2,1)}, bf16[2,64,16,4,128]{4,3,2,1,0:T(4,128)(2,1)}) fusion(bf16[2,64,16,4,128]{4,3,2,1,0:T(4,128)(2,1)} %param.23, pred[64,16]{1,0:T(8,128)(4,1)} %iota_compare_fusion, bf16[2,64,4,128]{3,2,1,0:T(4,128)(2,1)S(1)} %broadcast_in_dim.34, bf16[2,64,16,4,128]{4,3,2,1,0:T(4,128)(2,1)} %param.22, ...), kind=kLoop, calls=%fused_computation | loop fusion | flops 2097152 | bytes 8651776 | tf_op jit(solution)/shard_map/jit(_where)/select_n | solution.py:519
  202.7 0.0 copy-done
  202.7 0.7 copy.25
Async XLA Ops:
  196.2 6.5 %copy-start = (bf16[64,2048]{1,0:T(8,128)(2,1)S(1)}, bf16[64,2048]{1,0:T(8,128)(2,1)}, u32[]{:S(2)}) copy-start(bf16[64,2048]{1,0:T(8,128)(2,1)} %get-tuple-element.14) | copy-start | bytes 786436

commit v2 on v1

--- a/solution.py
+++ b/solution.py
@@ -14,7 +14,8 @@
 RMS_EPS = 1e-5
 ROPE_BASE = 10000.0
 CB = 512
-SLOTS = 15
+SLOTS = 18
+PAIR = 2
 
 
 def rms_scale(v):
@@ -25,14 +26,18 @@
     return jnp.dot(a, b, preferred_element_type=F32)
 
 
+def dot_t1(a, b):
+    return lax.dot_general(a, b, (((1,), (1,)), ((), ())), preferred_element_type=F32)
+
+
 def dot_t0(a, b):
     return lax.dot_general(a, b, (((0,), (0,)), ((), ())), preferred_element_type=F32)
 
 
 def step_kernel(dims, hid, pos, ids, kc, vc, wq, wk, wv, wo, ag, qg, kg, mg, wr, wg, wu, wd, ctab, stab,
-                out, kn, vn,
-                ring, rsem, ssem, posv, idsv, agv, qgv, kgv, mgv, ctv, stv, xcur, hbuf, qf, kf, vf, mx,
-                kcv, vcv, posb, cosb, sinb, rk, xg, xd, act, yb, cb, part, prt, far, comb, near, wrv, knb, vnb,
+                out, ko, vo,
+                ring, rsem, ssem, posv, idsv, agv, qgv, kgv, mgv, ctv, stv, xcur, hbuf, qf, kf, vf, mf,
+                kcv, vcv, posb, cosb, sinb, rk, xg, xd, act, yb, cb, part, prt, far, comb, near, wrv,
                 rkss, rkrs, agss, agrs, rsss, rsrs, osem):
     n_layers, n_ep, T, D, QW, KVW, HD, S, E, EL, F, CAP = dims
     KV = KVW // HD
@@ -80,22 +85,22 @@
 
             @pl.when(r < NQ)
             def _():
-                pltpu.make_async_copy(wq.at[l, :, cols(r)], dst, sem).start()
+                pltpu.make_async_copy(wq.at[l, :, cols(r)], dst, sem).start(priority=1)
 
             @pl.when(r == NQ)
             def _():
-                pltpu.make_async_copy(wk.at[l], dst, sem).start()
+                pltpu.make_async_copy(wk.at[l], dst, sem).start(priority=1)
 
             @pl.when(r == NQ + 1)
             def _():
-                pltpu.make_async_copy(wv.at[l], dst, sem).start()
+                pltpu.make_async_copy(wv.at[l], dst, sem).start(priority=1)
 
             @pl.when((r >= O_AT) & (r < G_AT))
             def _():
                 j = r - O_AT
                 half = lax.rem(j, QW // D)
                 rows = pl.ds(pl.multiple_of(half * D, D), D)
-                pltpu.make_async_copy(wo.at[l, rows, cols(j // (QW // D))], dst, sem).start()
+                pltpu.make_async_copy(wo.at[l, rows, cols(j // (QW // D))], dst, sem).start(priority=1)
 
             @pl.when((r >= G_AT) & (r < D_AT))
             def _():
@@ -105,22 +110,22 @@
 
                 @pl.when(piece == 0)
                 def _():
-                    pltpu.make_async_copy(wg.at[e, :, 0:CB], dst, sem).start()
+                    pltpu.make_async_copy(wg.at[e, :, 0:CB], dst, sem).start(priority=1)
 
                 @pl.when(piece == 1)
                 def _():
-                    pltpu.make_async_copy(wu.at[e, :, 0:CB], dst, sem).start()
+                    pltpu.make_async_copy(wu.at[e, :, 0:CB], dst, sem).start(priority=1)
 
                 @pl.when(piece == 2)
                 def _():
-                    pltpu.make_async_copy(wg.at[e, :, CB:F], ring.at[slot_rows(k), 0:CF], sem).start()
-                    pltpu.make_async_copy(wu.at[e, :, CB:F], ring.at[slot_rows(k), CF:CB], sem).start()
+                    pltpu.make_async_copy(wg.at[e, :, CB:F], ring.at[slot_rows(k), 0:CF], sem).start(priority=1)
+                    pltpu.make_async_copy(wu.at[e, :, CB:F], ring.at[slot_rows(k), CF:CB], sem).start(priority=1)
 
             @pl.when(r >= D_AT)
             def _():
                 j = r - D_AT
                 rows = pl.ds(pl.multiple_of(lax.rem(j, ND1) * D, D), D)
-                pltpu.make_async_copy(wd.at[rows, cols(j // ND1)], dst, sem).start()
+                pltpu.make_async_copy(wd.at[rows, cols(j // ND1)], dst, sem).start(priority=1)
 
     def arrive(k):
         pltpu.make_async_copy(wk.at[0], ring.at[slot_rows(k)], rsem.at[lax.rem(k, SLOTS)]).wait()
@@ -145,7 +150,9 @@
     for cp in small_copies:
         cp.wait()
 
-    posf = jnp.broadcast_to(posv[...].astype(F32), (T, HD))
+    eye = lax.broadcasted_iota(jnp.int32, (T, T), 0) == lax.broadcasted_iota(jnp.int32, (T, T), 1)
+    posc = jnp.sum(jnp.where(eye, jnp.broadcast_to(posv[...].astype(F32), (T, T)), 0.0), axis=1, keepdims=True)
+    posf = jnp.broadcast_to(posc, (T, HD))
     posb[...] = posf
     cos = jnp.zeros((T, HD), F32)
     sin = jnp.zeros((T, HD), F32)
@@ -156,16 +163,18 @@
     cosb[...] = cos
     sinb[...] = sin
 
-    lane_e = lax.broadcasted_iota(jnp.int32, (T, E), 1)
-    tril = (lax.broadcasted_iota(jnp.int32, (T, T), 0) > lax.broadcasted_iota(jnp.int32, (T, T), 1))
-    tril = jnp.where(tril, 1.0, 0.0).astype(BF16)
+    row_e = lax.broadcasted_iota(jnp.int32, (E, T), 0)
+    earlier = lax.broadcasted_iota(jnp.int32, (T, T), 0) < lax.broadcasted_iota(jnp.int32, (T, T), 1)
+    earlier = jnp.where(earlier, 1.0, 0.0).astype(BF16)
+    eye = jnp.where(eye, 1.0, 0.0).astype(BF16)
     for l in range(n_layers):
         idl = idsv[l]
-        chosen = jnp.zeros((T, E), F32)
-        for j in range(idl.shape[1]):
-            chosen = jnp.where(idl[:, j:j + 1] == lane_e, 1.0, chosen)
-        rank = dot(tril, chosen.astype(BF16))
-        rk[me, :, l * E:(l + 1) * E] = jnp.where(chosen > 0.5, rank, -1.0).astype(BF16)
+        chosen = jnp.zeros((E, T), F32)
+        for j in range(idl.shape[0]):
+            chosen = jnp.where(idl[j:j + 1, :] == row_e, 1.0, chosen)
+        rank = dot(chosen.astype(BF16), earlier)
+        rank = jnp.where(chosen > 0.5, rank, -1.0).astype(BF16)
+        rk[me, :, l * E:(l + 1) * E] = dot_t1(eye, rank).astype(BF16)
 
     pl.semaphore_wait(barrier, 3)
 
@@ -192,19 +201,17 @@
             cp(opp, 3, nxt).wait_recv()
             cp(opp, 6, partner).start()
 
-        def finish():
-            for kind in (0, 4, 5, 6):
-                cp(me, kind, partner).wait_recv()
+        def landed(kind):
+            cp(me, kind, partner).wait_recv()
+
+        def sent():
             for kind in range(7):
                 cp(me, kind, partner).wait_send()
 
-        return own, forward, across, finish
-
-    own, forward, across, finish = gather_stages(lambda b: rk.at[b], lambda i: rkss.at[i], lambda i: rkrs.at[i])
-    own()
-    forward()
-    across()
-    finish()
+        return own, forward, across, landed, sent
+
+    rk_own, rk_forward, rk_across, rk_landed, rk_sent = gather_stages(lambda b: rk.at[b], lambda i: rkss.at[i], lambda i: rkrs.at[i])
+    rk_own()
 
     for cp in big_copies:
         cp.wait()
@@ -236,56 +243,59 @@
         vf[...] = dot(hbuf[...], ring[slot_rows(base + NQ + 1), :])
         issue(base + NQ + 1 + SLOTS)
 
-        def attend(g, c):
-            rows = pl.ds(pl.multiple_of(g * 8, 8), 8)
-            crows = pl.ds(pl.multiple_of(g * GR, GR), GR)
-            cos8 = cosb[rows, :]
-            sin8 = sinb[rows, :]
-            pos8 = posb[rows, :]
-
-            def rope(t):
-                return t * cos8 + pltpu.roll(t, HD // 2, 1) * sin8
-
-            q8 = qf[rows, :]
-            q8 = q8 * rms_scale(q8) * qgv[pl.ds(l, 1), :]
-            qs = jnp.concatenate([rope(q8[:, h * HD:(h + 1) * HD]) for h in range(H)], axis=0).astype(BF16)
-            k8 = kf[rows, :]
-            k8 = k8 * rms_scale(k8) * kgv[pl.ds(l, 1), :]
-            k_tiles = [rope(k8[:, h * HD:(h + 1) * HD]) for h in range(KV)]
-            kf[rows, :] = jnp.concatenate(k_tiles, axis=1)
-            v8 = vf[rows, :]
-            v_tiles = [v8[:, h * HD:(h + 1) * HD] for h in range(KV)]
-            fresh = jnp.concatenate([jnp.concatenate(k_tiles, axis=0), jnp.concatenate(v_tiles, axis=0), jnp.ones((8 * KV, HD), F32)], axis=1).astype(BF16)
-            posw = jnp.concatenate([pos8] * (GR // HD), axis=1)
-            hit8 = diag & (col_s == posw)
-            ok8 = diag & (col_s <= posw)
-            place = jnp.concatenate([jnp.where(hit8 & (col_kv == h), 1.0, 0.0) for h in range(KV)], axis=0).astype(BF16)
-            okay = jnp.concatenate([jnp.where(ok8 & (col_kv == h), 1.0, 0.0)[None, None] for h in range(KV)], axis=0)
-            put = dot_t0(place, fresh)
-            hits = put[:, 2 * HD:] > 0.5
-            kb = jnp.where(hits, put[:, :HD], kcv[l, crows, :].astype(F32)).astype(BF16)
-            vb = jnp.where(hits, put[:, HD:2 * HD], vcv[l, crows, :].astype(F32)).astype(BF16)
-            sc = lax.dot_general(qs, kb, (((1,), (1,)), ((), ())), preferred_element_type=F32) * (HD ** -0.5)
-            sc = sc.reshape(KV, HG, 8, GR)
-            sc = jnp.where(jnp.broadcast_to(okay, sc.shape) > 0.5, sc, -1e30).reshape(H * 8, GR)
-            ex = jnp.exp(sc - jnp.max(sc, axis=-1, keepdims=True))
-            pr = (ex * (1.0 / jnp.sum(ex, axis=-1, keepdims=True))).astype(BF16)
-            mixed = dot(pr, vb)
-            qf[rows, :] = jnp.concatenate([mixed[h * 8:(h + 1) * 8, :] for h in range(H)], axis=1)
+        @pl.when(l == 0)
+        def _():
+            rk_forward()
+
+        def attend(i, c):
+            groups = [i * PAIR + u for u in range(PAIR)]
+            rows = [pl.ds(pl.multiple_of(g * 8, 8), 8) for g in groups]
+            crows = [pl.ds(pl.multiple_of(g * GR, GR), GR) for g in groups]
+            loads = [(qf[r, :], kf[r, :], vf[r, :], cosb[r, :], sinb[r, :], posb[r, :], kcv[l, cr, :], vcv[l, cr, :]) for r, cr in zip(rows, crows)]
+            qgain = qgv[pl.ds(l, 1), :]
+            kgain = kgv[pl.ds(l, 1), :]
+            done = []
+            for q8, k8, v8, cos8, sin8, pos8, kold, vold in loads:
+                def rope(t):
+                    return t * cos8 + pltpu.roll(t, HD // 2, 1) * sin8
+
+                q8 = q8 * rms_scale(q8) * qgain
+                qs = jnp.concatenate([rope(q8[:, h * HD:(h + 1) * HD]) for h in range(H)], axis=0).astype(BF16)
+                k8 = k8 * rms_scale(k8) * kgain
+                k_tiles = [rope(k8[:, h * HD:(h + 1) * HD]) for h in range(KV)]
+                v_tiles = [v8[:, h * HD:(h + 1) * HD] for h in range(KV)]
+                fresh = jnp.concatenate([jnp.concatenate(k_tiles, axis=0), jnp.concatenate(v_tiles, axis=0), jnp.ones((8 * KV, HD), F32)], axis=1).astype(BF16)
+                posw = jnp.concatenate([pos8] * (GR // HD), axis=1)
+                hit8 = diag & (col_s == posw)
+                ok8 = diag & (col_s <= posw)
+                place = jnp.concatenate([jnp.where(hit8 & (col_kv == h), 1.0, 0.0) for h in range(KV)], axis=0).astype(BF16)
+                put = dot_t0(place, fresh)
+                hits = put[:, 2 * HD:] > 0.5
+                kb = jnp.where(hits, put[:, :HD], kold.astype(F32)).astype(BF16)
+                vb = jnp.where(hits, put[:, HD:2 * HD], vold.astype(F32)).astype(BF16)
+                sc = dot_t1(qs, kb)
+                parts = []
+                for h in range(KV):
+                    okay = jnp.where(ok8 & (col_kv == h), 1.0, 0.0)[None]
+                    sh = sc[h * HG * 8:(h + 1) * HG * 8].reshape(HG, 8, GR)
+                    sh = jnp.where(jnp.broadcast_to(okay, sh.shape) > 0.5, sh * (HD ** -0.5), -1e30).reshape(HG * 8, GR)
+                    ex = jnp.exp(sh - jnp.max(sh, axis=-1, keepdims=True))
+                    parts.append((ex * (1.0 / jnp.sum(ex, axis=-1, keepdims=True))).astype(BF16))
+                mixed = dot(jnp.concatenate(parts, axis=0), vb)
+                done.append((jnp.concatenate([mixed[h * 8:(h + 1) * 8, :] for h in range(H)], axis=1), kb, vb))
+            for r, cr, (m8, kb, vb) in zip(rows, crows, done):
+                mf[r, :] = m8
+                kcv[l, cr, :] = kb
+                vcv[l, cr, :] = vb
             return c
 
-        lax.fori_loop(0, T // 8, attend, 0)
-        mx[...] = qf[...].astype(BF16)
-
-        @pl.when(l > 0)
+        lax.fori_loop(0, T // 8 // PAIR, attend, 0)
+        pltpu.make_async_copy(kcv.at[l], ko.at[l], osem.at[l, 0]).start()
+        pltpu.make_async_copy(vcv.at[l], vo.at[l], osem.at[l, 1]).start()
+
+        @pl.when(l == 0)
         def _():
-            pltpu.make_async_copy(knb, kn.at[0], osem.at[0]).wait()
-            pltpu.make_async_copy(vnb, vn.at[0], osem.at[1]).wait()
-
-        knb[...] = kf[...].astype(BF16)
-        vnb[...] = vf[...].astype(BF16)
-        pltpu.make_async_copy(knb, kn.at[l], osem.at[0]).start()
-        pltpu.make_async_copy(vnb, vn.at[l], osem.at[1]).start()
+            rk_across()
 
         stages = []
         for n in range(NCH):
@@ -298,7 +308,7 @@
             for half in range(QW // D):
                 k = base + O_AT + n * (QW // D) + half
                 arrive(k)
-                term = dot(mx[:, half * D:(half + 1) * D], ring[slot_rows(k), :])
+                term = dot(mf[:, half * D:(half + 1) * D].astype(BF16), ring[slot_rows(k), :])
                 total = term if total is None else total + term
                 issue(k + SLOTS)
             xn = (acc + total).astype(BF16)
@@ -309,12 +319,6 @@
                 stages[n - 1][1]()
             if n >= 2:
                 stages[n - 2][2]()
-        stages[NCH - 1][1]()
-        stages[NCH - 2][2]()
-        stages[NCH - 1][2]()
-        for n in range(NCH):
-            stages[n][3]()
-
         lane = lax.broadcasted_iota(jnp.int32, (E, EL * 2 * CAP), 1)
         expand = jnp.where(lax.broadcasted_iota(jnp.int32, (E, EL * 2 * CAP), 0) == me * EL + lane // (2 * CAP), 1.0, 0.0).astype(BF16)
         lane_t = lax.broadcasted_iota(jnp.int32, (2 * T, EL * 2 * CAP), 1)
@@ -322,7 +326,37 @@
         lane_c = lax.rem(lane_t, CAP).astype(F32)
         lcol = pl.ds(pl.multiple_of(l * E, E), E)
 
-        def route(xc, c):
+        def route(i, c):
+            @pl.when(i == 0)
+            def _():
+                for n in range(NCH):
+                    stages[n][3](0)
+
+                @pl.when(l == 0)
+                def _():
+                    for kind in (0, 4, 5, 6):
+                        rk_landed(kind)
+                    rk_sent()
+
+            @pl.when(i == 1)
+            def _():
+                stages[NCH - 1][1]()
+                for n in range(NCH):
+                    stages[n][3](4)
+
+            @pl.when(i == 2)
+            def _():
+                stages[NCH - 2][2]()
+                for n in range(NCH):
+                    stages[n][3](5)
+
+            @pl.when(i == 3)
+            def _():
+                stages[NCH - 1][2]()
+                for n in range(NCH):
+                    stages[n][3](6)
+
+            xc = jnp.where(i == 0, chip, jnp.where(i == 1, nchip, jnp.where(i == 2, pchip, ochip)))
             xp = xg[pl.ds(xc * 2, 2)].reshape(2 * T, D).astype(F32)
             hp = (xp * rms_scale(xp) * mgv[pl.ds(l, 1), :]).astype(BF16)
             logits = dot(hp, wrv[...])
@@ -343,6 +377,8 @@
             return c
 
         lax.fori_loop(0, NX, route, 0)
+        for n in range(NCH):
+            stages[n][4]()
 
         def gate_up(e, c):
             k = base + G_AT + 3 * e
@@ -450,10 +486,11 @@
         return carry
 
     lax.fori_loop(0, n_layers, layer, 0)
-    last = pltpu.make_async_copy(xcur, out, osem.at[2])
+    last = pltpu.make_async_copy(xcur, out, ssem.at[0])
     last.start()
-    pltpu.make_async_copy(knb, kn.at[0], osem.at[0]).wait()
-    pltpu.make_async_copy(vnb, vn.at[0], osem.at[1]).wait()
+    for l in range(n_layers):
+        pltpu.make_async_copy(kcv.at[l], ko.at[l], osem.at[l, 0]).wait()
+        pltpu.make_async_copy(vcv.at[l], vo.at[l], osem.at[l, 1]).wait()
     last.wait()
 
 
@@ -489,10 +526,10 @@
         DMA = pltpu.SemaphoreType.DMA
         scratch = [
             V((SLOTS * D, CB), BF16), DMA((SLOTS,)), DMA((12,)),
-            V((T, 1), jnp.int32), V((L, T, top_k), jnp.int32),
+            V((1, T), jnp.int32), V((L, top_k, T), jnp.int32),
             V((L, D), F32), V((L, QW), F32), V((L, KVW), F32), V((L, D), F32),
             V((S, HD), F32), V((S, HD), F32),
-            V((T, D), BF16), V((T, D), BF16), V((T, QW), F32), V((T, KVW), F32), V((T, KVW), F32), V((T, QW), BF16),
+            V((T, D), BF16), V((T, D), BF16), V((T, QW), F32), V((T, KVW), F32), V((T, KVW), F32), V((T, QW), F32),
             V((L, rows, HD), BF16), V((L, rows, HD), BF16),
             V((T, HD), F32), V((T, HD), F32), V((T, HD), F32),
             V((n_ep, T, L * E), BF16), V((n_ep, T, D), BF16),
@@ -500,24 +537,21 @@
             V((NX, EL * 2 * CAP, CB), BF16), V((NX, 6 * T, EL * 2 * CAP), BF16),
             V((NCH, 2, NX, T, CB), F32), V((NCH, NX, T, CB), F32),
             V((NCH, T, CB), F32), V((NCH, T, CB), F32), V((NCH, T, CB), F32),
-            V((D, E), BF16), V((T, KVW), BF16), V((T, KVW), BF16),
-            DMA((7,)), DMA((7,)), DMA((NCH, 7)), DMA((NCH, 7)), DMA((NCH, 4)), DMA((NCH, 4)), DMA((3,)),
+            V((D, E), BF16),
+            DMA((7,)), DMA((7,)), DMA((NCH, 7)), DMA((NCH, 7)), DMA((NCH, 4)), DMA((NCH, 4)), DMA((L, 2)),
         ]
-        out, kn, vn = pl.pallas_call(
+        out, ko, vo = pl.pallas_call(
             functools.partial(step_kernel, dims),
-            out_shape=(jax.ShapeDtypeStruct((T, D), BF16), jax.ShapeDtypeStruct((L, T, KVW), BF16), jax.ShapeDtypeStruct((L, T, KVW), BF16)),
+            out_shape=(jax.ShapeDtypeStruct((T, D), BF16), jax.ShapeDtypeStruct((L, rows, HD), BF16), jax.ShapeDtypeStruct((L, rows, HD), BF16)),
             in_specs=[anyspec] * 19,
             out_specs=(anyspec,) * 3,
             scratch_shapes=scratch,
             compiler_params=pltpu.CompilerParams(collective_id=0, has_side_effects=True, vmem_limit_bytes=67043328),
             name="moe_decode",
-        )(hidden, positions.reshape(T, 1), expert_ids, k_cache.reshape(L, rows, HD), v_cache.reshape(L, rows, HD),
+        )(hidden, positions.reshape(1, T), expert_ids.transpose(0, 2, 1), k_cache.reshape(L, rows, HD), v_cache.reshape(L, rows, HD),
           w_query, w_key, w_value, w_out, attn_gain, q_gain, k_gain, mlp_gain, w_router, w_gate, w_up,
           w_down.reshape(EL * F, D), jnp.asarray(ctab), jnp.asarray(stab))
-        hit = (jnp.arange(S)[None, :] == positions[:, None])[None, :, :, None, None]
-        k_new = jnp.where(hit, kn.reshape(L, T, 1, KV, HD), k_cache)
-        v_new = jnp.where(hit, vn.reshape(L, T, 1, KV, HD), v_cache)
-        return out, k_new, v_new
+        return out, ko.reshape(k_cache.shape), vo.reshape(v_cache.shape)
 
     row_spec = P(batch_axes, None)
     cache_spec = P(None, batch_axes, None, None, None)

time: 204 us -> 182 us (0.89)
  Pallas kernels: 190 us -> 174 us
  other arithmetic: 7.86 us -> 0 us
    pallas_call x1, Pallas kernels: 190 us -> 174 us  [device_step(): pl.pallas_call(functools.partial(step_kernel, dims), out_shape=(jax.Shape...]
    select_n x1 -> x0, other arithmetic: 6.54 us -> none  [device_step(): v_new = jnp.where(hit, vn.reshape(L, T, 1, KV, HD), v_cache)]
    unnamed x4 -> x5, local copies, waits for them, and re-layouts: 2.13 us -> 7.07 us
where the time goes in v2:
time: 182 us
  Pallas kernels  174 us (96%)
  local copies, waits for them, and re-layouts  7.07 us (4%)
    pallas_call x1, Pallas kernels, device_step(): pl.pallas_call(functools.partial(step_kernel, dims), out_shape=(jax.Shape...  174 us
    unnamed x5, local copies, waits for them, and re-layouts  7.07 us

profile of v2, /device:TPU:82, one launch (start us, length us, event | category | flops | bytes accessed | tf_op | source)
XLA Modules:
  0.0 181.6 jit_solution(8017604546452547638)
XLA Ops:
  0.6 173.9 %moe_decode.1 = (bf16[64,2048]{1,0:T(8,128)(2,1)}, bf16[2,4096,128]{2,1,0:T(8,128)(2,1)}, bf16[2,4096,128]{2,1,0:T(8,128)(2,1)}) custom-call(bf16[64,2048]{1,0:T(8,128)(2,1)} %hid.1, s32[1,64]{1,0:T(1,128)} %bitcast.13, s32[2,8,64]{2,1,0:T(8,128)} %bitcast.12, bf16[2,4096,128]{2,1,0:T(8,128)(2,1)} %bitcast.8, bf16[2,4096,128]{2,1,0:T(8,128)(2,1)} %bitcast.9, ...), custom_call_target="tpu_custom_call" | custom-call | tf_op jit(solution)/shard_map/moe_decode/pallas_call | solution.py:543
  174.5 0.0 copy-start
  174.5 1.8 %copy.25 = bf16[64,2048]{1,0:T(8,128)(2,1)} copy(bf16[64,2048]{1,0:T(8,128)(2,1)} %get-tuple-element.12) | data formatting | bytes 524288
  176.4 3.9 %copy.26 = bf16[2,64,16,4,128]{4,3,2,1,0:T(4,128)(2,1)} copy(bf16[2,64,16,4,128]{4,3,2,1,0:T(4,128)(2,1)} %bitcast.11) | data formatting | bytes 4194304
  180.3 0.0 copy-done
  180.3 1.3 copy.27
Async XLA Ops:
  174.5 5.8 %copy-start = (bf16[2,4096,128]{2,1,0:T(8,128)(2,1)S(1)}, bf16[2,4096,128]{2,1,0:T(8,128)(2,1)}, u32[]{:S(2)}) copy-start(bf16[2,4096,128]{2,1,0:T(8,128)(2,1)} %get-tuple-element.8) | copy-start | bytes 6291460

commit v3 on v2

--- a/solution.py
+++ b/solution.py
@@ -14,8 +14,9 @@
 RMS_EPS = 1e-5
 ROPE_BASE = 10000.0
 CB = 512
+RB = 256
 SLOTS = 18
-PAIR = 2
+PAIR = 4
 
 
 def rms_scale(v):
@@ -38,7 +39,7 @@
                 out, ko, vo,
                 ring, rsem, ssem, posv, idsv, agv, qgv, kgv, mgv, ctv, stv, xcur, hbuf, qf, kf, vf, mf,
                 kcv, vcv, posb, cosb, sinb, rk, xg, xd, act, yb, cb, part, prt, far, comb, near, wrv,
-                rkss, rkrs, agss, agrs, rsss, rsrs, osem):
+                rkss, rkrs, agss, agrs, rsss, rsrs, osem, csem):
     n_layers, n_ep, T, D, QW, KVW, HD, S, E, EL, F, CAP = dims
     KV = KVW // HD
     H = QW // HD
@@ -48,8 +49,9 @@
     NQ = QW // CB
     NO = NCH * (QW // D)
     NGU = 3 * EL
-    ND1 = EL * F // D
-    ND = NCH * ND1
+    NR = D // RB
+    ND1 = EL * F // (2 * D)
+    ND = NR * ND1
     O_AT = NQ + 2
     G_AT = O_AT + NO
     D_AT = G_AT + NGU
@@ -124,8 +126,10 @@
             @pl.when(r >= D_AT)
             def _():
                 j = r - D_AT
-                rows = pl.ds(pl.multiple_of(lax.rem(j, ND1) * D, D), D)
-                pltpu.make_async_copy(wd.at[rows, cols(j // ND1)], dst, sem).start(priority=1)
+                rcols = pl.ds(pl.multiple_of(j // ND1 * RB, RB), RB)
+                for half in range(2):
+                    rows = pl.ds(pl.multiple_of((half * ND1 + lax.rem(j, ND1)) * D, D), D)
+                    pltpu.make_async_copy(wd.at[rows, rcols], ring.at[slot_rows(k), half * RB:(half + 1) * RB], sem).start(priority=1)
 
     def arrive(k):
         pltpu.make_async_copy(wk.at[0], ring.at[slot_rows(k)], rsem.at[lax.rem(k, SLOTS)]).wait()
@@ -139,10 +143,18 @@
         issue(k)
         return carry
 
-    lax.fori_loop(0, SLOTS, prime, 0)
-    big_copies = [pltpu.make_async_copy(a, b, ssem.at[len(smalls) + i]) for i, (a, b) in enumerate(((kc, kcv), (vc, vcv), (wr, wrv)))]
-    for cp in big_copies:
+    def cache_copies(l):
+        return (pltpu.make_async_copy(kc.at[l], kcv.at[l], csem.at[l, 0]), pltpu.make_async_copy(vc.at[l], vcv.at[l], csem.at[l, 1]))
+
+    router_copy = pltpu.make_async_copy(wr, wrv, ssem.at[len(smalls)])
+    lax.fori_loop(0, O_AT, prime, 0)
+    for cp in cache_copies(0):
         cp.start()
+    router_copy.start()
+    lax.fori_loop(O_AT, SLOTS, prime, 0)
+    for l in range(1, n_layers):
+        for cp in cache_copies(l):
+            cp.start()
 
     barrier = pltpu.get_barrier_semaphore()
     for dev in (partner, nxt, prv):
@@ -213,9 +225,6 @@
     rk_own, rk_forward, rk_across, rk_landed, rk_sent = gather_stages(lambda b: rk.at[b], lambda i: rkss.at[i], lambda i: rkrs.at[i])
     rk_own()
 
-    for cp in big_copies:
-        cp.wait()
-
     col = lax.broadcasted_iota(jnp.int32, (8, S * KV * 8), 1)
     col_b = col // (S * KV)
     col_s = lax.rem(col // KV, S).astype(F32)
@@ -229,19 +238,24 @@
         hbuf[...] = (x * rms_scale(x) * agv[pl.ds(l, 1), :]).astype(BF16)
 
         def q_step(j, c):
-            k = base + j
+            k = base + 2 * j
             arrive(k)
-            qf[:, pl.ds(pl.multiple_of(j * CB, CB), CB)] = dot(hbuf[...], ring[slot_rows(k), :])
+            arrive(k + 1)
+            for u in range(2):
+                qf[:, pl.ds(pl.multiple_of((2 * j + u) * CB, CB), CB)] = dot(hbuf[...], ring[slot_rows(k + u), :])
             issue(k + SLOTS)
+            issue(k + 1 + SLOTS)
             return c
 
-        lax.fori_loop(0, NQ, q_step, 0)
+        lax.fori_loop(0, NQ // 2, q_step, 0)
         arrive(base + NQ)
+        arrive(base + NQ + 1)
         kf[...] = dot(hbuf[...], ring[slot_rows(base + NQ), :])
+        vf[...] = dot(hbuf[...], ring[slot_rows(base + NQ + 1), :])
         issue(base + NQ + SLOTS)
-        arrive(base + NQ + 1)
-        vf[...] = dot(hbuf[...], ring[slot_rows(base + NQ + 1), :])
         issue(base + NQ + 1 + SLOTS)
+        for cp in cache_copies(l):
+            cp.wait()
 
         @pl.when(l == 0)
         def _():
@@ -306,8 +320,9 @@
             acc = xcur[:, cs].astype(F32)
             total = None
             for half in range(QW // D):
+                arrive(base + O_AT + n * (QW // D) + half)
+            for half in range(QW // D):
                 k = base + O_AT + n * (QW // D) + half
-                arrive(k)
                 term = dot(mf[:, half * D:(half + 1) * D].astype(BF16), ring[slot_rows(k), :])
                 total = term if total is None else total + term
                 issue(k + SLOTS)
@@ -337,6 +352,7 @@
                     for kind in (0, 4, 5, 6):
                         rk_landed(kind)
                     rk_sent()
+                    router_copy.wait()
 
             @pl.when(i == 1)
             def _():
@@ -424,28 +440,23 @@
         def stage3(n):
             send_near(n).wait_recv()
             send_comb(n).wait_recv()
-            cs = pl.ds(pl.multiple_of(n * CB, CB), CB)
+            cs = pl.ds(pl.multiple_of(n * RB, RB), RB)
             total = part[n, core, chip] + comb[n] + near[n]
             xcur[:, cs] = (xcur[:, cs].astype(F32) + total).astype(BF16)
 
         def down(n, c):
-            def piece(i, cc):
-                k = base + D_AT + n * ND1 + 3 * i
-                for j in range(3):
-                    arrive(k + j)
-                row0 = lax.rem(k, SLOTS) * D
-                per = 3 * D // F
-                for m in range(per):
-                    e = i * per + m
-                    wrows = pl.ds(pl.multiple_of(row0 + m * F, 256), F)
-                    y = dot(act[e], ring[wrows, :]).astype(BF16)
-                    for xc in range(NX):
-                        yb[xc, pl.ds(pl.multiple_of(e * 2 * CAP, 2 * CAP), 2 * CAP), :] = y[xc * 2 * CAP:(xc + 1) * 2 * CAP, :]
-                for j in range(3):
-                    issue(k + j + SLOTS)
-                return cc
-
-            lax.fori_loop(0, ND1 // 3, piece, 0)
+            k = base + D_AT + ND1 * n
+            for j in range(ND1):
+                arrive(k + j)
+            row0 = lax.rem(k, SLOTS) * D
+            per = EL // 2
+            for e in range(EL):
+                wrows = pl.ds(pl.multiple_of(row0 + (e % per) * F, 256), F)
+                y = dot(act[e], ring[wrows, e // per * RB:(e // per + 1) * RB]).astype(BF16)
+                for xc in range(NX):
+                    yb[xc, e * 2 * CAP:(e + 1) * 2 * CAP, :] = y[xc * 2 * CAP:(xc + 1) * 2 * CAP, :]
+            for j in range(ND1):
+                issue(k + j + SLOTS)
             for xc in range(NX):
                 p3 = dot(cb[xc], yb[xc])
                 p1 = p3[:2 * T] + (p3[2 * T:4 * T] + p3[4 * T:])
@@ -457,23 +468,31 @@
             def _():
                 stage1(n - 1)
 
-            @pl.when(n >= 2)
-            def _():
-                stage2(n - 2)
-
             @pl.when(n >= 3)
             def _():
-                stage3(n - 3)
+                stage2(n - 3)
+
+            @pl.when(n >= 5)
+            def _():
+                stage3(n - 5)
 
             return c
 
-        lax.fori_loop(0, NCH, down, 0)
-        stage1(NCH - 1)
-        stage2(NCH - 2)
-        stage3(NCH - 3)
-        stage2(NCH - 1)
-        stage3(NCH - 2)
-        stage3(NCH - 1)
+        lax.fori_loop(0, NR, down, 0)
+        stage1(NR - 1)
+
+        def tail(n, c):
+            @pl.when(n < NR)
+            def _():
+                stage2(n)
+
+            @pl.when(n - 2 < NR)
+            def _():
+                stage3(n - 2)
+
+            return c
+
+        lax.fori_loop(NR - 3, NR + 2, tail, 0)
 
         def drain(n, c):
             send0(n).wait_send()
@@ -482,7 +501,7 @@
             send_comb(n).wait_send()
             return c
 
-        lax.fori_loop(0, NCH, drain, 0)
+        lax.fori_loop(0, NR, drain, 0)
         return carry
 
     lax.fori_loop(0, n_layers, layer, 0)
@@ -492,6 +511,26 @@
         pltpu.make_async_copy(kcv.at[l], ko.at[l], osem.at[l, 0]).wait()
         pltpu.make_async_copy(vcv.at[l], vo.at[l], osem.at[l, 1]).wait()
     last.wait()
+
+
+def hand_over(out_in, k_in, v_in, out, k_out, v_out, obuf, kbuf, vbuf, isem, osem):
+    pieces = []
+    for l in range(k_in.shape[0]):
+        quarter = k_in.shape[1] // 4
+        for q in range(4):
+            rows = pl.ds(q * quarter, quarter)
+            pieces.append((k_in.at[l, rows], kbuf.at[l, rows], k_out.at[l, rows]))
+            pieces.append((v_in.at[l, rows], vbuf.at[l, rows], v_out.at[l, rows]))
+    pieces.append((out_in, obuf, out))
+    loads = [pltpu.make_async_copy(a, b, isem.at[i]) for i, (a, b, _) in enumerate(pieces)]
+    stores = [pltpu.make_async_copy(b, c, osem.at[i]) for i, (_, b, c) in enumerate(pieces)]
+    for cp in loads:
+        cp.start()
+    for ld, st in zip(loads, stores):
+        ld.wait()
+        st.start()
+    for st in stores:
+        st.wait()
 
 
 def rope_tables(cache_len, head_dim):
@@ -534,11 +573,11 @@
             V((T, HD), F32), V((T, HD), F32), V((T, HD), F32),
             V((n_ep, T, L * E), BF16), V((n_ep, T, D), BF16),
             V((EL, n_ep * CAP, D), BF16), V((EL, n_ep * CAP, F), BF16),
-            V((NX, EL * 2 * CAP, CB), BF16), V((NX, 6 * T, EL * 2 * CAP), BF16),
-            V((NCH, 2, NX, T, CB), F32), V((NCH, NX, T, CB), F32),
-            V((NCH, T, CB), F32), V((NCH, T, CB), F32), V((NCH, T, CB), F32),
+            V((NX, EL * 2 * CAP, RB), BF16), V((NX, 6 * T, EL * 2 * CAP), BF16),
+            V((D // RB, 2, NX, T, RB), F32), V((D // RB, NX, T, RB), F32),
+            V((D // RB, T, RB), F32), V((D // RB, T, RB), F32), V((D // RB, T, RB), F32),
             V((D, E), BF16),
-            DMA((7,)), DMA((7,)), DMA((NCH, 7)), DMA((NCH, 7)), DMA((NCH, 4)), DMA((NCH, 4)), DMA((L, 2)),
+            DMA((7,)), DMA((7,)), DMA((NCH, 7)), DMA((NCH, 7)), DMA((D // RB, 4)), DMA((D // RB, 4)), DMA((L, 2)), DMA((L, 2)),
         ]
         out, ko, vo = pl.pallas_call(
             functools.partial(step_kernel, dims),
@@ -551,6 +590,14 @@
         )(hidden, positions.reshape(1, T), expert_ids.transpose(0, 2, 1), k_cache.reshape(L, rows, HD), v_cache.reshape(L, rows, HD),
           w_query, w_key, w_value, w_out, attn_gain, q_gain, k_gain, mlp_gain, w_router, w_gate, w_up,
           w_down.reshape(EL * F, D), jnp.asarray(ctab), jnp.asarray(stab))
+        out, ko, vo = pl.pallas_call(
+            hand_over,
+            out_shape=tuple(jax.ShapeDtypeStruct(a.shape, BF16) for a in (out, ko, vo)),
+            in_specs=[anyspec] * 3,
+            out_specs=(anyspec,) * 3,
+            scratch_shapes=[V((T, D), BF16), V((L, rows, HD), BF16), V((L, rows, HD), BF16), DMA((17,)), DMA((17,))],
+            name="hand_over",
+        )(out, ko, vo)
         return out, ko.reshape(k_cache.shape), vo.reshape(v_cache.shape)
 
     row_spec = P(batch_axes, None)

time: 182 us -> 172 us (0.945)
  local copies, waits for them, and re-layouts: 7.07 us -> 0 us
  Pallas kernels: 174 us -> 171 us
    unnamed x5 -> x0, local copies, waits for them, and re-layouts: 7.07 us -> none
    pallas_call x1, Pallas kernels: 174 us -> 167 us  [device_step(): pl.pallas_call(functools.partial(step_kernel, dims), out_shape=(jax.Shape...]
    pallas_call x0 -> x1, Pallas kernels: none -> 4.14 us  [device_step(): pl.pallas_call(hand_over, out_shape=tuple((jax.ShapeDtypeStruct(a.shape,...]
where the time goes in v3:
time: 172 us
  Pallas kernels  171 us (99%)
    pallas_call x1, Pallas kernels, device_step(): pl.pallas_call(functools.partial(step_kernel, dims), out_shape=(jax.Shape...  167 us
    pallas_call x1, Pallas kernels, device_step(): pl.pallas_call(hand_over, out_shape=tuple((jax.ShapeDtypeStruct(a.shape,...  4.14 us

profile of v3, /device:TPU:82, one launch (start us, length us, event | category | flops | bytes accessed | tf_op | source)
XLA Modules:
  0.0 171.6 jit_solution(13353713949773618404)
XLA Ops:
  0.6 166.8 %moe_decode.1 = (bf16[64,2048]{1,0:T(8,128)(2,1)}, bf16[2,4096,128]{2,1,0:T(8,128)(2,1)}, bf16[2,4096,128]{2,1,0:T(8,128)(2,1)}) custom-call(bf16[64,2048]{1,0:T(8,128)(2,1)} %hid.1, s32[1,64]{1,0:T(1,128)} %bitcast.11, s32[2,8,64]{2,1,0:T(8,128)} %bitcast.10, bf16[2,4096,128]{2,1,0:T(8,128)(2,1)} %bitcast.8, bf16[2,4096,128]{2,1,0:T(8,128)(2,1)} %bitcast.9, ...), custom_call_target="tpu_custom_call" | custom-call | tf_op jit(solution)/shard_map/moe_decode/pallas_call | solution.py:582
  167.5 4.1 %hand_over.1 = (bf16[64,2048]{1,0:T(8,128)(2,1)}, bf16[2,4096,128]{2,1,0:T(8,128)(2,1)}, bf16[2,4096,128]{2,1,0:T(8,128)(2,1)}) custom-call(bf16[64,2048]{1,0:T(8,128)(2,1)} %get-tuple-element.9.out_in, bf16[2,4096,128]{2,1,0:T(8,128)(2,1)} %get-tuple-element.10.k_in, bf16[2,4096,128]{2,1,0:T(8,128)(2,1)} %get-tuple-element.11.v_in), custom_call_target="tpu_custom_call" | custom-call | tf_op jit(solution)/shard_map/hand_over/pallas_call | solution.py:593

commit v4 on v3

--- a/solution.py
+++ b/solution.py
@@ -17,6 +17,7 @@
 RB = 256
 SLOTS = 18
 PAIR = 4
+PIECES = 4
 
 
 def rms_scale(v):
@@ -36,8 +37,8 @@
 
 
 def step_kernel(dims, hid, pos, ids, kc, vc, wq, wk, wv, wo, ag, qg, kg, mg, wr, wg, wu, wd, ctab, stab,
-                out, ko, vo,
-                ring, rsem, ssem, posv, idsv, agv, qgv, kgv, mgv, ctv, stv, xcur, hbuf, qf, kf, vf, mf,
+                out, kn, vn,
+                ring, rsem, ssem, posv, idsv, agv, qgv, kgv, mgv, ctv, stv, xcur, hbuf, qf, kf, vf, knb, vnb,
                 kcv, vcv, posb, cosb, sinb, rk, xg, xd, act, yb, cb, part, prt, far, comb, near, wrv,
                 rkss, rkrs, agss, agrs, rsss, rsrs, osem, csem):
     n_layers, n_ep, T, D, QW, KVW, HD, S, E, EL, F, CAP = dims
@@ -144,7 +145,7 @@
         return carry
 
     def cache_copies(l):
-        return (pltpu.make_async_copy(kc.at[l], kcv.at[l], csem.at[l, 0]), pltpu.make_async_copy(vc.at[l], vcv.at[l], csem.at[l, 1]))
+        return (pltpu.make_async_copy(kc.at[l], kcv, csem.at[0]), pltpu.make_async_copy(vc.at[l], vcv, csem.at[1]))
 
     router_copy = pltpu.make_async_copy(wr, wrv, ssem.at[len(smalls)])
     lax.fori_loop(0, O_AT, prime, 0)
@@ -152,10 +153,6 @@
         cp.start()
     router_copy.start()
     lax.fori_loop(O_AT, SLOTS, prime, 0)
-    for l in range(1, n_layers):
-        for cp in cache_copies(l):
-            cp.start()
-
     barrier = pltpu.get_barrier_semaphore()
     for dev in (partner, nxt, prv):
         pl.semaphore_signal(barrier, inc=1, device_id={"ep": dev}, device_id_type=MESH)
@@ -231,6 +228,9 @@
     col_kv = lax.rem(col, KV)
     diag = col_b == lax.broadcasted_iota(jnp.int32, (8, S * KV * 8), 0)
     GR = 8 * S * KV
+    o_row = lax.broadcasted_iota(jnp.int32, (8 * KV, 8 * KV), 0)
+    o_col = lax.broadcasted_iota(jnp.int32, (8 * KV, 8 * KV), 1)
+    order = jnp.where((o_row // KV == lax.rem(o_col, 8)) & (lax.rem(o_row, KV) == o_col // 8), 1.0, 0.0).astype(BF16)
 
     def layer(l, carry):
         base = l * TOT
@@ -265,7 +265,8 @@
             groups = [i * PAIR + u for u in range(PAIR)]
             rows = [pl.ds(pl.multiple_of(g * 8, 8), 8) for g in groups]
             crows = [pl.ds(pl.multiple_of(g * GR, GR), GR) for g in groups]
-            loads = [(qf[r, :], kf[r, :], vf[r, :], cosb[r, :], sinb[r, :], posb[r, :], kcv[l, cr, :], vcv[l, cr, :]) for r, cr in zip(rows, crows)]
+            nrows = [pl.ds(pl.multiple_of(g * 8 * KV, 8 * KV), 8 * KV) for g in groups]
+            loads = [(qf[r, :], kf[r, :], vf[r, :], cosb[r, :], sinb[r, :], posb[r, :], kcv[cr, :], vcv[cr, :]) for r, cr in zip(rows, crows)]
             qgain = qgv[pl.ds(l, 1), :]
             kgain = kgv[pl.ds(l, 1), :]
             done = []
@@ -278,34 +279,48 @@
                 k8 = k8 * rms_scale(k8) * kgain
                 k_tiles = [rope(k8[:, h * HD:(h + 1) * HD]) for h in range(KV)]
                 v_tiles = [v8[:, h * HD:(h + 1) * HD] for h in range(KV)]
-                fresh = jnp.concatenate([jnp.concatenate(k_tiles, axis=0), jnp.concatenate(v_tiles, axis=0), jnp.ones((8 * KV, HD), F32)], axis=1).astype(BF16)
+                kall = jnp.concatenate(k_tiles, axis=0).astype(BF16)
+                vall = jnp.concatenate(v_tiles, axis=0).astype(BF16)
+                fresh = dot(order, jnp.concatenate([kall, vall], axis=1)).astype(BF16)
+                kall = kall.astype(F32)
+                vall = vall.astype(F32)
                 posw = jnp.concatenate([pos8] * (GR // HD), axis=1)
-                hit8 = diag & (col_s == posw)
-                ok8 = diag & (col_s <= posw)
-                place = jnp.concatenate([jnp.where(hit8 & (col_kv == h), 1.0, 0.0) for h in range(KV)], axis=0).astype(BF16)
-                put = dot_t0(place, fresh)
-                hits = put[:, 2 * HD:] > 0.5
-                kb = jnp.where(hits, put[:, :HD], kold.astype(F32)).astype(BF16)
-                vb = jnp.where(hits, put[:, HD:2 * HD], vold.astype(F32)).astype(BF16)
-                sc = dot_t1(qs, kb)
+                past8 = diag & (col_s < posw)
+                sc = dot_t1(qs, kold)
+                qsf = qs.astype(F32)
                 parts = []
+                adds = []
                 for h in range(KV):
-                    okay = jnp.where(ok8 & (col_kv == h), 1.0, 0.0)[None]
-                    sh = sc[h * HG * 8:(h + 1) * HG * 8].reshape(HG, 8, GR)
+                    hr = slice(h * HG * 8, (h + 1) * HG * 8)
+                    okay = jnp.where(past8 & (col_kv == h), 1.0, 0.0)[None]
+                    sh = sc[hr].reshape(HG, 8, GR)
                     sh = jnp.where(jnp.broadcast_to(okay, sh.shape) > 0.5, sh * (HD ** -0.5), -1e30).reshape(HG * 8, GR)
-                    ex = jnp.exp(sh - jnp.max(sh, axis=-1, keepdims=True))
-                    parts.append((ex * (1.0 / jnp.sum(ex, axis=-1, keepdims=True))).astype(BF16))
-                mixed = dot(jnp.concatenate(parts, axis=0), vb)
-                done.append((jnp.concatenate([mixed[h * 8:(h + 1) * 8, :] for h in range(H)], axis=1), kb, vb))
-            for r, cr, (m8, kb, vb) in zip(rows, crows, done):
-                mf[r, :] = m8
-                kcv[l, cr, :] = kb
-                vcv[l, cr, :] = vb
+                    knew = kall[h * 8:(h + 1) * 8][None]
+                    vnew = vall[h * 8:(h + 1) * 8][None]
+                    nh = jnp.sum(qsf[hr].reshape(HG, 8, HD) * knew, axis=-1, keepdims=True).reshape(HG * 8, 1) * (HD ** -0.5)
+                    top = jnp.maximum(jnp.max(sh, axis=-1, keepdims=True), nh)
+                    ex = jnp.exp(sh - top)
+                    en = jnp.exp(nh - top)
+                    inv = 1.0 / (jnp.sum(ex, axis=-1, keepdims=True) + en)
+                    parts.append((ex * inv).astype(BF16))
+                    pn = jnp.broadcast_to((en * inv).astype(BF16).astype(F32), (HG * 8, HD))
+                    adds.append((pn.reshape(HG, 8, HD) * vnew).reshape(HG * 8, HD))
+                mixed = dot(jnp.concatenate(parts, axis=0), vold) + jnp.concatenate(adds, axis=0)
+                done.append((jnp.concatenate([mixed[h * 8:(h + 1) * 8, :] for h in range(H)], axis=1), fresh))
+            for r, nr, (m8, fresh) in zip(rows, nrows, done):
+                qf[r, :] = m8
+                knb[l, nr, :] = fresh[:, :HD]
+                vnb[l, nr, :] = fresh[:, HD:]
             return c
 
         lax.fori_loop(0, T // 8 // PAIR, attend, 0)
-        pltpu.make_async_copy(kcv.at[l], ko.at[l], osem.at[l, 0]).start()
-        pltpu.make_async_copy(vcv.at[l], vo.at[l], osem.at[l, 1]).start()
+        pltpu.make_async_copy(knb.at[l], kn.at[l], osem.at[l, 0]).start()
+        pltpu.make_async_copy(vnb.at[l], vn.at[l], osem.at[l, 1]).start()
+
+        @pl.when(l + 1 < n_layers)
+        def _():
+            for cp in cache_copies(l + 1):
+                cp.start()
 
         @pl.when(l == 0)
         def _():
@@ -323,7 +338,7 @@
                 arrive(base + O_AT + n * (QW // D) + half)
             for half in range(QW // D):
                 k = base + O_AT + n * (QW // D) + half
-                term = dot(mf[:, half * D:(half + 1) * D].astype(BF16), ring[slot_rows(k), :])
+                term = dot(qf[:, half * D:(half + 1) * D].astype(BF16), ring[slot_rows(k), :])
                 total = term if total is None else total + term
                 issue(k + SLOTS)
             xn = (acc + total).astype(BF16)
@@ -508,26 +523,32 @@
     last = pltpu.make_async_copy(xcur, out, ssem.at[0])
     last.start()
     for l in range(n_layers):
-        pltpu.make_async_copy(kcv.at[l], ko.at[l], osem.at[l, 0]).wait()
-        pltpu.make_async_copy(vcv.at[l], vo.at[l], osem.at[l, 1]).wait()
+        pltpu.make_async_copy(knb.at[l], kn.at[l], osem.at[l, 0]).wait()
+        pltpu.make_async_copy(vnb.at[l], vn.at[l], osem.at[l, 1]).wait()
     last.wait()
 
 
-def hand_over(out_in, k_in, v_in, out, k_out, v_out, obuf, kbuf, vbuf, isem, osem):
-    pieces = []
+def hand_over(pos, out_in, k_in, v_in, k_fresh, v_fresh, out, k_out, v_out, obuf, kbuf, vbuf, knew, vnew, isem, osem):
+    span = k_in.shape[1] // PIECES
+    fresh = [pltpu.make_async_copy(k_fresh, knew, isem.at[0]), pltpu.make_async_copy(v_fresh, vnew, isem.at[1])]
+    jobs = [(out_in, obuf, out, None)]
     for l in range(k_in.shape[0]):
-        quarter = k_in.shape[1] // 4
-        for q in range(4):
-            rows = pl.ds(q * quarter, quarter)
-            pieces.append((k_in.at[l, rows], kbuf.at[l, rows], k_out.at[l, rows]))
-            pieces.append((v_in.at[l, rows], vbuf.at[l, rows], v_out.at[l, rows]))
-    pieces.append((out_in, obuf, out))
-    loads = [pltpu.make_async_copy(a, b, isem.at[i]) for i, (a, b, _) in enumerate(pieces)]
-    stores = [pltpu.make_async_copy(b, c, osem.at[i]) for i, (_, b, c) in enumerate(pieces)]
-    for cp in loads:
+        for q in range(PIECES):
+            seqs = pl.ds(q * span, span)
+            jobs.append((k_in.at[l, seqs], kbuf.at[l, seqs], k_out.at[l, seqs], (kbuf, knew, l, q)))
+            jobs.append((v_in.at[l, seqs], vbuf.at[l, seqs], v_out.at[l, seqs], (vbuf, vnew, l, q)))
+    loads = [pltpu.make_async_copy(a, b, isem.at[2 + i]) for i, (a, b, _, _) in enumerate(jobs)]
+    stores = [pltpu.make_async_copy(b, c, osem.at[i]) for i, (_, b, c, _) in enumerate(jobs)]
+    for cp in fresh + loads:
         cp.start()
-    for ld, st in zip(loads, stores):
+    for cp in fresh:
+        cp.wait()
+    for ld, st, (_, _, _, patch) in zip(loads, stores, jobs):
         ld.wait()
+        if patch is not None:
+            buf, new, l, q = patch
+            for b in range(q * span, (q + 1) * span):
+                buf[l, b, pos[b]] = new[l, b]
         st.start()
     for st in stores:
         st.wait()
@@ -568,8 +589,8 @@
             V((1, T), jnp.int32), V((L, top_k, T), jnp.int32),
             V((L, D), F32), V((L, QW), F32), V((L, KVW), F32), V((L, D), F32),
             V((S, HD), F32), V((S, HD), F32),
-            V((T, D), BF16), V((T, D), BF16), V((T, QW), F32), V((T, KVW), F32), V((T, KVW), F32), V((T, QW), F32),
-            V((L, rows, HD), BF16), V((L, rows, HD), BF16),
+            V((T, D), BF16), V((T, D), BF16), V((T, QW), F32), V((T, KVW), F32), V((T, KVW), F32), V((L, T * KV, HD), BF16), V((L, T * KV, HD), BF16),
+            V((rows, HD), BF16), V((rows, HD), BF16),
             V((T, HD), F32), V((T, HD), F32), V((T, HD), F32),
             V((n_ep, T, L * E), BF16), V((n_ep, T, D), BF16),
             V((EL, n_ep * CAP, D), BF16), V((EL, n_ep * CAP, F), BF16),
@@ -577,11 +598,11 @@
             V((D // RB, 2, NX, T, RB), F32), V((D // RB, NX, T, RB), F32),
             V((D // RB, T, RB), F32), V((D // RB, T, RB), F32), V((D // RB, T, RB), F32),
             V((D, E), BF16),
-            DMA((7,)), DMA((7,)), DMA((NCH, 7)), DMA((NCH, 7)), DMA((D // RB, 4)), DMA((D // RB, 4)), DMA((L, 2)), DMA((L, 2)),
+            DMA((7,)), DMA((7,)), DMA((NCH, 7)), DMA((NCH, 7)), DMA((D // RB, 4)), DMA((D // RB, 4)), DMA((L, 2)), DMA((2,)),
         ]
-        out, ko, vo = pl.pallas_call(
+        out, kn, vn = pl.pallas_call(
             functools.partial(step_kernel, dims),
-            out_shape=(jax.ShapeDtypeStruct((T, D), BF16), jax.ShapeDtypeStruct((L, rows, HD), BF16), jax.ShapeDtypeStruct((L, rows, HD), BF16)),
+            out_shape=(jax.ShapeDtypeStruct((T, D), BF16), jax.ShapeDtypeStruct((L, T * KV, HD), BF16), jax.ShapeDtypeStruct((L, T * KV, HD), BF16)),
             in_specs=[anyspec] * 19,
             out_specs=(anyspec,) * 3,
             scratch_shapes=scratch,
@@ -590,15 +611,16 @@
         )(hidden, positions.reshape(1, T), expert_ids.transpose(0, 2, 1), k_cache.reshape(L, rows, HD), v_cache.reshape(L, rows, HD),
           w_query, w_key, w_value, w_out, attn_gain, q_gain, k_gain, mlp_gain, w_router, w_gate, w_up,
           w_down.reshape(EL * F, D), jnp.asarray(ctab), jnp.asarray(stab))
-        out, ko, vo = pl.pallas_call(
+        n_copies = 2 * L * PIECES + 3
+        return pl.pallas_call(
             hand_over,
-            out_shape=tuple(jax.ShapeDtypeStruct(a.shape, BF16) for a in (out, ko, vo)),
-            in_specs=[anyspec] * 3,
+            out_shape=tuple(jax.ShapeDtypeStruct(a.shape, BF16) for a in (out, k_cache, v_cache)),
+            in_specs=[pl.BlockSpec(memory_space=pltpu.SMEM)] + [anyspec] * 5,
             out_specs=(anyspec,) * 3,
-            scratch_shapes=[V((T, D), BF16), V((L, rows, HD), BF16), V((L, rows, HD), BF16), DMA((17,)), DMA((17,))],
+            scratch_shapes=[V((T, D), BF16), V(k_cache.shape, BF16), V(v_cache.shape, BF16), V((L, T, KV, HD), BF16), V((L, T, KV, HD), BF16),
+                            DMA((n_copies,)), DMA((n_copies,))],
             name="hand_over",
-        )(out, ko, vo)
-        return out, ko.reshape(k_cache.shape), vo.reshape(v_cache.shape)
+        )(positions, out, k_cache, v_cache, kn.reshape(L, T, KV, HD), vn.reshape(L, T, KV, HD))
 
     row_spec = P(batch_axes, None)
     cache_spec = P(None, batch_axes, None, None, None)

time: 172 us -> 169 us (0.983)
  Pallas kernels: 171 us -> 167 us
    pallas_call x1, Pallas kernels: 167 us -> 162 us  [device_step(): pl.pallas_call(functools.partial(step_kernel, dims), out_shape=(jax.Shape...]
where the time goes in v4:
time: 169 us; the launch traced here: 168 us
  Pallas kernels  167 us (99%)
    pallas_call x1, Pallas kernels, device_step(): pl.pallas_call(functools.partial(step_kernel, dims), out_shape=(jax.Shape...  162 us
    pallas_call x1, Pallas kernels, device_step(): pl.pallas_call(hand_over, out_shape=tuple((jax.ShapeDtypeStruct(a.shape,...  4.96 us

profile of v4, /device:TPU:82, one launch (start us, length us, event | category | flops | bytes accessed | tf_op | source)
XLA Modules:
  0.0 168.0 jit_solution(5648691561957637180)
XLA Ops:
  0.6 162.4 %moe_decode.1 = (bf16[64,2048]{1,0:T(8,128)(2,1)}, bf16[2,256,128]{2,1,0:T(8,128)(2,1)}, bf16[2,256,128]{2,1,0:T(8,128)(2,1)}) custom-call(bf16[64,2048]{1,0:T(8,128)(2,1)} %hid.1, s32[1,64]{1,0:T(1,128)} %bitcast.13, s32[2,8,64]{2,1,0:T(8,128)} %bitcast.12, bf16[2,4096,128]{2,1,0:T(8,128)(2,1)} %bitcast.8, bf16[2,4096,128]{2,1,0:T(8,128)(2,1)} %bitcast.9, ...), custom_call_target="tpu_custom_call" | custom-call | tf_op jit(solution)/shard_map/moe_decode/pallas_call | solution.py:603
  163.1 5.0 %hand_over.1 = (bf16[64,2048]{1,0:T(8,128)(2,1)}, bf16[2,64,16,4,128]{4,3,2,1,0:T(4,128)(2,1)}, bf16[2,64,16,4,128]{4,3,2,1,0:T(4,128)(2,1)}) custom-call(s32[64]{0:T(128)} %pos.1, bf16[64,2048]{1,0:T(8,128)(2,1)} %get-tuple-element.6.out_in, bf16[2,64,16,4,128]{4,3,2,1,0:T(4,128)(2,1)} %k_in.1, bf16[2,64,16,4,128]{4,3,2,1,0:T(4,128)(2,1)} %v_in.1, ...), custom_call_target="tpu_custom_call" | custom-call | tf_op jit(solution)/shard_map/hand_over/pallas_call | solution.py:615
